TPU v7x, 8 devices: a whole 2x2x1 slice. The times are simulated.
8 devices in a mesh: fsdp: 8 (over z, y, x, core).
Axes of the slice: x: 2, y: 2, z: 1, core: 2. Of those that a mesh axis runs over, the one named last changes fastest.
Arguments:
- hidden: bfloat16 [8, 1024, 1024], P('fsdp')
- positions: int32 [1024], replicated
- grad_out: bfloat16 [8, 1024, 1024], P('fsdp')
- ln_gain: bfloat16 [2, 1024], P(None, 'fsdp')
- ln_bias: bfloat16 [2, 1024], P(None, 'fsdp')
- w_query: bfloat16 [2, 1024, 16, 64], P(None, 'fsdp')
- b_query: bfloat16 [2, 1024], P(None, 'fsdp')
- w_key: bfloat16 [2, 1024, 16, 64], P(None, 'fsdp')
- b_key: bfloat16 [2, 1024], P(None, 'fsdp')
- w_value: bfloat16 [2, 1024, 16, 64], P(None, 'fsdp')
- b_value: bfloat16 [2, 1024], P(None, 'fsdp')
- w_out: bfloat16 [2, 1024, 1024], P(None, 'fsdp')
- b_out: bfloat16 [2, 1024], P(None, 'fsdp')
- w_up: bfloat16 [2, 1024, 4096], P(None, 'fsdp')
- b_up: bfloat16 [2, 4096], P(None, 'fsdp')
- w_down: bfloat16 [2, 4096, 1024], P(None, 'fsdp')
- b_down: bfloat16 [2, 1024], P(None, 'fsdp')
Outputs:
- output 1: bfloat16 [8, 1024, 1024], P('fsdp')
- output 2: bfloat16 [8, 1024, 1024], P('fsdp')
- output 3: float32 [2, 1024], P(None, 'fsdp')
- output 4: float32 [2, 1024], P(None, 'fsdp')
- output 5: float32 [2, 1024, 16, 64], P(None, 'fsdp')
- output 6: float32 [2, 1024], P(None, 'fsdp')
- output 7: float32 [2, 1024, 16, 64], P(None, 'fsdp')
- output 8: float32 [2, 1024], P(None, 'fsdp')
- output 9: float32 [2, 1024, 16, 64], P(None, 'fsdp')
- output 10: float32 [2, 1024], P(None, 'fsdp')
- output 11: float32 [2, 1024, 1024], P(None, 'fsdp')
- output 12: float32 [2, 1024], P(None, 'fsdp')
- output 13: float32 [2, 1024, 4096], P(None, 'fsdp')
- output 14: float32 [2, 4096], P(None, 'fsdp')
- output 15: float32 [2, 4096, 1024], P(None, 'fsdp')
- output 16: float32 [2, 1024], P(None, 'fsdp')
All inputs are finite; a program needn't handle non-finite values.
Results may differ from a plain program's by a relative error of at most 0.02.
Values are sent between devices in bfloat16 or wider.
A program may use at most 1 GiB of HBM per device.

v0:
```python
import jax
import jax.numpy as jnp
from jax import lax
from jax.sharding import PartitionSpec as P

ROT = 32
LN_EPS = 1e-5
THETA = 10000.0
AXIS_NAME = 'fsdp'
ALL_SLOTS = tuple(range(14))
BACKWARD_SLOTS = (0, 2, 4, 6, 8, 10, 12)


def rope_tables(positions):
    half_rot = ROT // 2
    inv_freq = THETA ** (-2.0 * jnp.arange(half_rot, dtype=jnp.float32) / ROT)
    angles = positions.astype(jnp.float32)[:, None] * inv_freq[None, :]
    return jnp.cos(angles)[:, None, :], jnp.sin(angles)[:, None, :]


def rotate(vectors, cos_t, sin_t, direction):
    half_rot = ROT // 2
    first = vectors[..., :half_rot]
    second = vectors[..., half_rot:ROT]
    return jnp.concatenate([first * cos_t - direction * second * sin_t, second * cos_t + direction * first * sin_t, vectors[..., ROT:]], axis=-1)


def gelu_tanh(values):
    return jax.nn.gelu(values, approximate=True)


def layer_forward(hidden, weights, cos_t, sin_t):
    (ln_gain, ln_bias, w_query, b_query, w_key, b_key, w_value, b_value, w_out, b_out, w_up, b_up, w_down, b_down) = weights
    n_seqs, seq_len, width = hidden.shape
    heads, head_dim = w_query.shape[1], w_query.shape[2]
    tok_f32 = hidden.reshape(n_seqs * seq_len, width).astype(jnp.float32)
    centred = tok_f32 - jnp.mean(tok_f32, axis=-1, keepdims=True)
    inv_std = lax.rsqrt(jnp.mean(centred * centred, axis=-1, keepdims=True) + LN_EPS)
    normed = centred * inv_std
    normed_bf = (normed * ln_gain.astype(jnp.float32) + ln_bias.astype(jnp.float32)).astype(jnp.bfloat16)

    def project(weight, bias_vec):
        heads_out = jnp.einsum('td,dhk->thk', normed_bf, weight, preferred_element_type=jnp.float32)
        return (heads_out + bias_vec.astype(jnp.float32).reshape(heads, head_dim)).reshape(n_seqs, seq_len, heads, head_dim)

    q_heads = rotate(project(w_query, b_query), cos_t, sin_t, 1.0).astype(jnp.bfloat16)
    k_heads = rotate(project(w_key, b_key), cos_t, sin_t, 1.0).astype(jnp.bfloat16)
    v_heads = project(w_value, b_value).astype(jnp.bfloat16)
    scores = jnp.einsum('bqhk,bshk->bhqs', q_heads, k_heads, preferred_element_type=jnp.float32) * head_dim ** -0.5
    causal = jnp.arange(seq_len)[:, None] >= jnp.arange(seq_len)[None, :]
    attn_probs = jax.nn.softmax(jnp.where(causal, scores, -1e30), axis=-1)
    mixed = jnp.einsum('bhqs,bshk->bqhk', attn_probs.astype(jnp.bfloat16), v_heads, preferred_element_type=jnp.float32)
    mixed = mixed.astype(jnp.bfloat16).reshape(n_seqs * seq_len, width)
    attn_out = jnp.dot(mixed, w_out, preferred_element_type=jnp.float32)
    up_pre = jnp.dot(normed_bf, w_up, preferred_element_type=jnp.float32) + b_up.astype(jnp.float32)
    up_act = gelu_tanh(up_pre).astype(jnp.bfloat16)
    mlp_out = jnp.dot(up_act, w_down, preferred_element_type=jnp.float32)
    new_hidden = tok_f32 + attn_out + b_out.astype(jnp.float32) + mlp_out + b_down.astype(jnp.float32)
    residuals = (normed, inv_std, normed_bf, q_heads, k_heads, v_heads, attn_probs, mixed, up_pre, up_act)
    return new_hidden.astype(jnp.bfloat16).reshape(n_seqs, seq_len, width), residuals


def layer_backward(grad_hidden, weights, residuals, cos_t, sin_t):
    (ln_gain, w_query, w_key, w_value, w_out, w_up, w_down) = weights
    (normed, inv_std, normed_bf, q_heads, k_heads, v_heads, attn_probs, mixed, up_pre, up_act) = residuals
    n_seqs, seq_len, heads, head_dim = q_heads.shape
    width = heads * head_dim
    tok_count = n_seqs * seq_len
    grad_tok = grad_hidden.reshape(tok_count, width)
    grad_f32 = grad_tok.astype(jnp.float32)
    grad_bias_out = jnp.sum(grad_f32, axis=0)

    grad_w_down = jnp.einsum('tf,td->fd', up_act, grad_tok, preferred_element_type=jnp.float32)
    grad_up = jnp.einsum('td,fd->tf', grad_tok, w_down, preferred_element_type=jnp.float32).astype(jnp.bfloat16)
    gelu_pull = jax.vjp(gelu_tanh, up_pre)[1]
    grad_pre = gelu_pull(grad_up.astype(jnp.float32))[0]
    grad_b_up = jnp.sum(grad_pre, axis=0)
    grad_pre_bf = grad_pre.astype(jnp.bfloat16)
    grad_w_up = jnp.einsum('td,tf->df', normed_bf, grad_pre_bf, preferred_element_type=jnp.float32)
    grad_normed = jnp.einsum('tf,df->td', grad_pre_bf, w_up, preferred_element_type=jnp.float32)

    grad_w_out = jnp.einsum('te,td->ed', mixed, grad_tok, preferred_element_type=jnp.float32)
    grad_mixed = jnp.einsum('td,ed->te', grad_tok, w_out, preferred_element_type=jnp.float32).astype(jnp.bfloat16)
    grad_mixed = grad_mixed.reshape(n_seqs, seq_len, heads, head_dim)
    grad_probs = jnp.einsum('bqhk,bshk->bhqs', grad_mixed, v_heads, preferred_element_type=jnp.float32)
    grad_value = jnp.einsum('bhqs,bqhk->bshk', attn_probs.astype(jnp.bfloat16), grad_mixed, preferred_element_type=jnp.float32)
    grad_scores = attn_probs * (grad_probs - jnp.sum(attn_probs * grad_probs, axis=-1, keepdims=True)) * head_dim ** -0.5
    grad_scores = grad_scores.astype(jnp.bfloat16)
    grad_query = rotate(jnp.einsum('bhqs,bshk->bqhk', grad_scores, k_heads, preferred_element_type=jnp.float32), cos_t, sin_t, -1.0)
    grad_key = rotate(jnp.einsum('bhqs,bqhk->bshk', grad_scores, q_heads, preferred_element_type=jnp.float32), cos_t, sin_t, -1.0)

    def head_grads(grad_heads, weight):
        flat = grad_heads.reshape(tok_count, heads, head_dim)
        bias_grad = jnp.sum(flat, axis=0).reshape(width)
        flat_bf = flat.astype(jnp.bfloat16)
        weight_grad = jnp.einsum('td,thk->dhk', normed_bf, flat_bf, preferred_element_type=jnp.float32)
        back_grad = jnp.einsum('thk,dhk->td', flat_bf, weight, preferred_element_type=jnp.float32)
        return weight_grad, bias_grad, back_grad

    query_wgrad, query_bgrad, query_back = head_grads(grad_query, w_query)
    key_wgrad, key_bgrad, key_back = head_grads(grad_key, w_key)
    value_wgrad, value_bgrad, value_back = head_grads(grad_value, w_value)
    grad_normed = grad_normed + query_back + key_back + value_back

    grad_gain = jnp.sum(grad_normed * normed, axis=0)
    grad_ln_bias = jnp.sum(grad_normed, axis=0)
    grad_hat = grad_normed * ln_gain.astype(jnp.float32)
    grad_norm_in = inv_std * (grad_hat - jnp.mean(grad_hat, axis=-1, keepdims=True) - normed * jnp.mean(grad_hat * normed, axis=-1, keepdims=True))
    grad_in = (grad_f32 + grad_norm_in).astype(jnp.bfloat16).reshape(n_seqs, seq_len, width)
    local_grads = (grad_gain, grad_ln_bias, query_wgrad, query_bgrad, key_wgrad, key_bgrad, value_wgrad, value_bgrad, grad_w_out, grad_bias_out, grad_w_up, grad_b_up, grad_w_down)
    return grad_in, local_grads


def solution(mesh):
    group_size = mesh.shape[AXIS_NAME]
    batch_spec = P(AXIS_NAME)
    param_specs = (P(None, AXIS_NAME),) * 14

    def gather(shards, layer_idx, slots):
        return tuple(lax.all_gather(shards[slot][layer_idx], AXIS_NAME, axis=0, tiled=True) for slot in slots)

    def step(hidden, positions, grad_out, *shards):
        cos_t, sin_t = rope_tables(positions)
        layers = shards[0].shape[0]
        token_total = hidden.shape[0] * hidden.shape[1] * group_size
        current = hidden
        saved_acts = []
        for layer_idx in range(layers):
            current, residuals = layer_forward(current, gather(shards, layer_idx, ALL_SLOTS), cos_t, sin_t)
            saved_acts.append(residuals)
        grad_cur = grad_out
        per_layer = [None] * layers
        for layer_idx in reversed(range(layers)):
            grad_cur, local_grads = layer_backward(grad_cur, gather(shards, layer_idx, BACKWARD_SLOTS), saved_acts[layer_idx], cos_t, sin_t)
            reduced = [lax.psum_scatter(grad_piece, AXIS_NAME, scatter_dimension=0, tiled=True) / token_total for grad_piece in local_grads]
            per_layer[layer_idx] = reduced + [reduced[9]]
        stacked = tuple(jnp.stack([per_layer[layer_pos][slot] for layer_pos in range(layers)]) for slot in ALL_SLOTS)
        return (current, grad_cur) + stacked

    return jax.shard_map(step, mesh=mesh, in_specs=(batch_spec, P(), batch_spec) + param_specs, out_specs=(batch_spec, batch_spec) + param_specs, check_vma=False)
```

profile of v0, /device:TPU:0, one launch (start us, length us, event | category | flops | bytes accessed | tf_op | source)
XLA Modules:
  0.0 1869.5 jit_solution(14978903832219884646)
XLA Ops:
  215.0 32.1 %fusion.297 = (f32[16,1024]{1,0:T(8,128)S(1)}, f32[16,1024,1024]{1,2,0:T(8,128)}) fusion(pred[1024,1024]{0,1:T(8,128)(4,1)S(1)} %iota_compare_fusion, bf16[1024,16,32]{0,2,1:T(8,128)(2,1)} %fusion.214, bf16[1024,16,16]{0,2,1:T(8,128)(2,1)} %get-tuple-element.117, bf16[1024,16,16]{0,2,1:T(8,128)(2,1)} %get-tuple-element.118, ...), kind=kOutput, calls=%fused_computation.370 | convolution fusion | flops 2227176448 | bytes 72417280 | tf_op jit(solution)/shard_map/sub | solution.py:51
  247.2 25.0 %fusion.196 = bf16[16,64,1024]{2,1,0:T(8,128)(2,1)} fusion(f32[1024,16,64]{0,2,1:T(8,128)} %bitcast.400, f32[16,64]{1,0:T(8,128)S(1)} %reshape.544, f32[16,1024,1024]{1,2,0:T(8,128)} %get-tuple-element.139, f32[16,1024]{1,0:T(8,128)S(1)} %get-tuple-element.138), kind=kOutput, calls=%fused_computation.225 | convolution fusion | flops 2184183808 | bytes 73469952 | tf_op jit(solution)/shard_map/bhqs,bshk->bqhk/dot_general | solution.py:52
  341.4 23.3 %fusion.218 = f32[16,1024,1024]{1,2,0:T(8,128)} fusion(bf16[1024,16,64]{0,2,1:T(8,128)(2,1)S(1)} %bitcast.414, f32[1024,16,64]{0,2,1:T(8,128)S(1)} %bitcast.402, f32[16,64]{1,0:T(8,128)S(1)} %copy-done.44), kind=kOutput, calls=%fused_computation.257 | convolution fusion | flops 2149580800 | bytes 73404416 | tf_op jit(solution)/shard_map/bqhk,bshk->bhqs/dot_general | solution.py:85
  364.7 31.9 %fusion.298 = (f32[16,1024]{1,0:T(8,128)S(1)}, f32[16,1024,1024]{1,2,0:T(8,128)}) fusion(pred[1024,1024]{0,1:T(8,128)(4,1)S(1)} %copy-done.31, bf16[1024,16,32]{0,2,1:T(8,128)(2,1)S(1)} %copy-done.34, bf16[1024,16,16]{0,2,1:T(8,128)(2,1)} %get-tuple-element.115, bf16[1024,16,16]{0,2,1:T(8,128)(2,1)} %get-tuple-element.116, ...), kind=kOutput, calls=%fused_computation.371 | convolution fusion | flops 2227176448 | bytes 72417280 | tf_op jit(solution)/shard_map/sub | solution.py:51
  396.5 82.9 %fusion.154 = f32[1,1024,16,64]{1,3,2,0:T(8,128)} fusion(f32[16,1024,1024]{1,2,0:T(8,128)} %fusion.218, bf16[1024,16,32]{0,2,1:T(8,128)(2,1)S(1)} %copy-done.34, bf16[1024,16,16]{0,2,1:T(8,128)(2,1)} %get-tuple-element.115, bf16[1024,16,16]{0,2,1:T(8,128)(2,1)} %get-tuple-element.116, f32[16,1024,1024]{1,2,0:T(8,128)} %get-tuple-element.143, ...), kind=kOutput, calls=%fused_computation.175 | convolution fusion | flops 2271233024 | bytes 140574720 | tf_op jit(solution)/shard_map/bhqs,bshk->bqhk/dot_general | solution.py:89
  479.5 83.1 %fusion.157 = f32[1,1024,16,64]{1,3,2,0:T(8,128)} fusion(f32[16,1024,1024]{1,2,0:T(8,128)} %fusion.218, bf16[1024,16,32]{0,2,1:T(8,128)(2,1)S(1)} %fusion.215, bf16[1024,16,16]{0,2,1:T(8,128)(2,1)} %get-tuple-element.89, bf16[1024,16,16]{0,2,1:T(8,128)(2,1)S(1)} %copy-done.40, f32[16,1024,1024]{1,2,0:T(8,128)} %get-tuple-element.143, ...), kind=kOutput, calls=%fused_computation.176 | convolution fusion | flops 2271233024 | bytes 140574720 | tf_op jit(solution)/shard_map/bhqs,bqhk->bshk/dot_general | solution.py:90
  573.2 26.3 %bitcast_convert_fusion = (bf16[1,1024,16,64]{1,3,2,0:T(8,128)(2,1)}, f32[16,64,1024]{2,1,0:T(8,128)}) fusion(bf16[1024,16,64]{0,2,1:T(8,128)(2,1)S(1)} %bitcast.415, f32[16,1024,1024]{1,2,0:T(8,128)} %get-tuple-element.143, f32[16,1024]{1,0:T(8,128)S(1)} %get-tuple-element.142), kind=kOutput, calls=%fused_computation.141 | convolution fusion | flops 2182086656 | bytes 75563008 | tf_op jit(solution)/shard_map/bhqs,bqhk->bshk/dot_general | solution.py:86
  630.6 25.0 %fusion.199 = bf16[16,64,1024]{2,1,0:T(8,128)(2,1)} fusion(f32[1024,16,64]{0,2,1:T(8,128)} %bitcast.403, f32[16,64]{1,0:T(8,128)S(1)} %copy-done.45, f32[16,1024,1024]{1,2,0:T(8,128)} %get-tuple-element.143, f32[16,1024]{1,0:T(8,128)S(1)} %get-tuple-element.142), kind=kOutput, calls=%fused_computation.226 | convolution fusion | flops 2184183808 | bytes 73469952 | tf_op jit(solution)/shard_map/bhqs,bshk->bqhk/dot_general | solution.py:52
  655.6 26.7 %fusion.299 = (f32[4096]{0:T(1024)}, bf16[1024,4096]{1,0:T(8,128)(2,1)}) fusion(f32[1024,4096]{1,0:T(8,128)} %fusion.62, f32[4096]{0:T(1024)S(1)} %bitcast.442, bf16[1,4096,1024]{2,1,0:T(8,128)(2,1)} %all-gather.63.cloned.1.call-done, bf16[1,1024,1024]{2,1,0:T(8,128)(2,1)} %param.19), kind=kOutput, calls=%fused_computation.372 | convolution fusion | flops 8690593792 | bytes 35684352 | tf_op jit(solution)/shard_map/td,fd->tf/dot_general | solution.py:74
  707.3 26.0 %bitcast_convert_fusion.1 = (bf16[1,1024,16,64]{1,3,2,0:T(8,128)(2,1)}, f32[16,64,1024]{2,1,0:T(8,128)}) fusion(bf16[1024,16,64]{0,2,1:T(8,128)(2,1)S(1)} %bitcast.416, f32[16,1024,1024]{1,2,0:T(8,128)} %get-tuple-element.139, f32[16,1024]{1,0:T(8,128)S(1)} %copy-done.97), kind=kOutput, calls=%fused_computation.143 | convolution fusion | flops 2182086656 | bytes 75563008 | tf_op jit(solution)/shard_map/bhqs,bqhk->bshk/dot_general | solution.py:86
  733.3 25.8 %fusion.217 = f32[16,1024,1024]{1,2,0:T(8,128)} fusion(bf16[1024,16,64]{0,2,1:T(8,128)(2,1)S(1)} %bitcast.417, f32[1024,16,64]{0,2,1:T(8,128)} %bitcast.401, f32[16,64]{1,0:T(8,128)S(1)} %copy-done.43), kind=kOutput, calls=%fused_computation.256 | convolution fusion | flops 2149580800 | bytes 73404416 | tf_op jit(solution)/shard_map/bqhk,bshk->bhqs/dot_general | solution.py:85
  759.1 83.0 %fusion.148 = f32[1,1024,16,64]{1,3,2,0:T(8,128)} fusion(f32[16,1024,1024]{1,2,0:T(8,128)} %fusion.217, bf16[1024,16,32]{0,2,1:T(8,128)(2,1)S(1)} %copy-done.33, bf16[1024,16,16]{0,2,1:T(8,128)(2,1)} %get-tuple-element.117, bf16[1024,16,16]{0,2,1:T(8,128)(2,1)} %get-tuple-element.118, f32[16,1024,1024]{1,2,0:T(8,128)} %get-tuple-element.139, ...), kind=kOutput, calls=%fused_computation.173 | convolution fusion | flops 2271233024 | bytes 140574720 | tf_op jit(solution)/shard_map/bhqs,bshk->bqhk/dot_general | solution.py:89
  842.1 83.2 %fusion.151 = f32[1,1024,16,64]{1,3,2,0:T(8,128)} fusion(f32[16,1024,1024]{1,2,0:T(8,128)} %fusion.217, bf16[1024,16,32]{0,2,1:T(8,128)(2,1)S(1)} %copy-done.32, bf16[1024,16,16]{0,2,1:T(8,128)(2,1)} %get-tuple-element.93, bf16[1024,16,16]{0,2,1:T(8,128)(2,1)S(1)} %copy-done.39, f32[16,1024,1024]{1,2,0:T(8,128)} %get-tuple-element.139, ...), kind=kOutput, calls=%fused_computation.174 | convolution fusion | flops 2271233024 | bytes 140574720 | tf_op jit(solution)/shard_map/bhqs,bqhk->bshk/dot_general | solution.py:90
  947.1 24.9 %fusion.300 = (f32[4096]{0:T(1024)}, bf16[1024,4096]{1,0:T(8,128)(2,1)}) fusion(f32[1024,4096]{1,0:T(8,128)} %fusion.70, f32[4096]{0:T(1024)S(1)} %bitcast.446, bf16[1024,1024]{0,1:T(8,128)(2,1)S(1)} %copy-done.5, bf16[1,4096,1024]{2,1,0:T(8,128)(2,1)} %all-gather.51.cloned.1.call-done), kind=kOutput, calls=%fused_computation.373 | convolution fusion | flops 8690593792 | bytes 35684352 | tf_op jit(solution)/shard_map/td,fd->tf/dot_general | solution.py:74
  1081.6 20.7 %fusion.259 = f32[4096,1024]{1,0:T(8,128)} fusion(bf16[1024,1024]{0,1:T(8,128)(2,1)} %copy-done.4, f32[1024,4096]{1,0:T(8,128)} %fusion.70, f32[4096]{0:T(1024)S(1)} %bitcast.447), kind=kOutput, calls=%fused_computation.346 | convolution fusion | flops 8631877632 | bytes 35667968 | tf_op jit(solution)/shard_map/tf,td->fd/dot_general | solution.py:73
  1213.6 20.1 %reduce-scatter.21.cloned.1.call-done = f32[128,16,64]{0,2,1:T(8,128)} async-done(((f32[1024,16,64]{0,2,1:T(8,128)}), f32[128,16,64]{0,2,1:T(8,128)}) %reduce-scatter.21.cloned.1.call-update) | async-done | bytes 524304 | tf_op jit(solution)/shard_map/reduce_scatter | solution.py:135
  1235.9 43.4 %reduce-scatter.19.cloned.1.call-done = f32[128,16,64]{0,2,1:T(8,128)} async-done(((f32[1024,16,64]{0,2,1:T(8,128)}), f32[128,16,64]{0,2,1:T(8,128)}) %reduce-scatter.19.cloned.1.call-update) | async-done | bytes 524304 | tf_op jit(solution)/shard_map/reduce_scatter | solution.py:135
  1280.4 44.7 %reduce-scatter.17.cloned.1.call-done = f32[128,16,64]{0,2,1:T(8,128)} async-done(((f32[1024,16,64]{0,2,1:T(8,128)}), f32[128,16,64]{0,2,1:T(8,128)}) %reduce-scatter.17.cloned.1.call-update) | async-done | bytes 524304 | tf_op jit(solution)/shard_map/reduce_scatter | solution.py:135
  1327.2 43.5 %reduce-scatter.15.cloned.1.call-done = f32[128,16,64]{0,2,1:T(8,128)} async-done(((f32[1024,16,64]{0,2,1:T(8,128)}), f32[128,16,64]{0,2,1:T(8,128)}) %reduce-scatter.15.cloned.1.call-update) | async-done | bytes 524304 | tf_op jit(solution)/shard_map/reduce_scatter | solution.py:135
  1371.7 44.7 %reduce-scatter.13.cloned.1.call-done = f32[128,16,64]{0,2,1:T(8,128)} async-done(((f32[1024,16,64]{0,2,1:T(8,128)}), f32[128,16,64]{0,2,1:T(8,128)}) %reduce-scatter.13.cloned.1.call-update) | async-done | bytes 524304 | tf_op jit(solution)/shard_map/reduce_scatter | solution.py:135
  1418.6 108.3 %reduce-scatter.35.cloned.1.call-done = f32[512,1024]{1,0:T(8,128)} async-done(((f32[4096,1024]{1,0:T(8,128)}), f32[512,1024]{1,0:T(8,128)}) %reduce-scatter.35.cloned.1.call-update) | async-done | bytes 2097168 | tf_op jit(solution)/shard_map/reduce_scatter | solution.py:135
  1528.7 108.7 %reduce-scatter.33.cloned.1.call-done = f32[512,1024]{1,0:T(8,128)} async-done(((f32[4096,1024]{1,0:T(8,128)}), f32[512,1024]{1,0:T(8,128)}) %reduce-scatter.33.cloned.1.call-update) | async-done | bytes 2097168 | tf_op jit(solution)/shard_map/reduce_scatter | solution.py:135
  1641.5 106.2 %reduce-scatter.31.cloned.1.call-done = f32[128,4096]{1,0:T(8,128)} async-done(((f32[1024,4096]{1,0:T(8,128)}), f32[128,4096]{1,0:T(8,128)}) %reduce-scatter.31.cloned.1.call-update) | async-done | bytes 2097168 | tf_op jit(solution)/shard_map/reduce_scatter | solution.py:135
  1749.5 108.7 %reduce-scatter.29.cloned.1.call-done = f32[128,4096]{1,0:T(8,128)} async-done(((f32[1024,4096]{1,0:T(8,128)}), f32[128,4096]{1,0:T(8,128)}) %reduce-scatter.29.cloned.1.call-update) | async-done | bytes 2097168 | tf_op jit(solution)/shard_map/reduce_scatter | solution.py:135
  (446 shorter events, 605.7 us)
Async XLA Ops:
  9.3 190.4 %all-gather.43.cloned.1.call-start = ((), (), s32[]{:S(2)}) async-start(), calls=%async_computation.25 | async-start | bytes 2359296 | tf_op jit(solution)/shard_map/all_gather | solution.py:120
  11.2 194.5 %all-gather.45.cloned.1.call-start = ((), (), s32[]{:S(2)}) async-start(), calls=%async_computation.26 | async-start | bytes 2359296 | tf_op jit(solution)/shard_map/all_gather | solution.py:120
  13.1 259.0 %all-gather.59.cloned.1.call-start = ((), (), s32[]{:S(2)}) async-start(), calls=%async_computation.33 | async-start | bytes 2359296 | tf_op jit(solution)/shard_map/all_gather | solution.py:120
  14.1 264.0 %all-gather.47.cloned.1.call-start = ((), (), s32[]{:S(2)}) async-start(), calls=%async_computation.27 | async-start | bytes 2359296 | tf_op jit(solution)/shard_map/all_gather | solution.py:120
  14.6 270.1 %all-gather.49.cloned.1.call-start = ((), (), s32[]{:S(2)}) async-start(), calls=%async_computation.28 | async-start | bytes 9437184 | tf_op jit(solution)/shard_map/all_gather | solution.py:120
  16.3 283.8 %all-gather.51.cloned.1.call-start = ((), (), s32[]{:S(2)}) async-start(), calls=%async_computation.29 | async-start | bytes 9437184 | tf_op jit(solution)/shard_map/all_gather | solution.py:120
  19.4 301.0 %all-gather.55.cloned.1.call-start = ((), (), s32[]{:S(2)}) async-start(), calls=%async_computation.31 | async-start | bytes 2359296 | tf_op jit(solution)/shard_map/all_gather | solution.py:120
  20.1 307.6 %all-gather.57.cloned.1.call-start = ((), (), s32[]{:S(2)}) async-start(), calls=%async_computation.32 | async-start | bytes 2359296 | tf_op jit(solution)/shard_map/all_gather | solution.py:120
  20.9 316.3 %all-gather.53.cloned.1.call-start = ((), (), s32[]{:S(2)}) async-start(), calls=%async_computation.30 | async-start | bytes 2359296 | tf_op jit(solution)/shard_map/all_gather | solution.py:120
  21.5 593.7 %all-gather.61.cloned.1.call-start = ((), (), s32[]{:S(2)}) async-start(), calls=%async_computation.34 | async-start | bytes 9437184 | tf_op jit(solution)/shard_map/all_gather | solution.py:120
  22.2 633.4 %all-gather.63.cloned.1.call-start = ((), (), s32[]{:S(2)}) async-start(), calls=%async_computation.35 | async-start | bytes 9437184 | tf_op jit(solution)/shard_map/all_gather | solution.py:120
  22.8 1172.5 %all-reduce.17.cloned.1.call-start = ((), (), s32[]{:S(2)}) async-start(), calls=%async_computation.36 | async-start | bytes 163840
  1005.4 203.9 %reduce-scatter.27.cloned.1.call-start = ((), (), s32[]{:S(2)}) async-start(), calls=%async_computation.19 | async-start | bytes 4718592 | tf_op jit(solution)/shard_map/reduce_scatter | solution.py:135
  1012.5 197.9 %reduce-scatter.25.cloned.1.call-start = ((), (), s32[]{:S(2)}) async-start(), calls=%async_computation.18 | async-start | bytes 4718592 | tf_op jit(solution)/shard_map/reduce_scatter | solution.py:135
  1019.1 193.4 %reduce-scatter.23.cloned.1.call-start = ((), (), s32[]{:S(2)}) async-start(), calls=%async_computation.17 | async-start | bytes 4718592 | tf_op jit(solution)/shard_map/reduce_scatter | solution.py:135
  1026.6 207.1 %reduce-scatter.21.cloned.1.call-start = ((), (), s32[]{:S(2)}) async-start(), calls=%async_computation.16 | async-start | bytes 4718592 | tf_op jit(solution)/shard_map/reduce_scatter | solution.py:135
  1033.4 245.9 %reduce-scatter.19.cloned.1.call-start = ((), (), s32[]{:S(2)}) async-start(), calls=%async_computation.15 | async-start | bytes 4718592 | tf_op jit(solution)/shard_map/reduce_scatter | solution.py:135
  1040.2 284.8 %reduce-scatter.17.cloned.1.call-start = ((), (), s32[]{:S(2)}) async-start(), calls=%async_computation.14 | async-start | bytes 4718592 | tf_op jit(solution)/shard_map/reduce_scatter | solution.py:135
  1047.2 323.4 %reduce-scatter.15.cloned.1.call-start = ((), (), s32[]{:S(2)}) async-start(), calls=%async_computation.13 | async-start | bytes 4718592 | tf_op jit(solution)/shard_map/reduce_scatter | solution.py:135
  1054.0 362.4 %reduce-scatter.13.cloned.1.call-start = ((), (), s32[]{:S(2)}) async-start(), calls=%async_computation.12 | async-start | bytes 4718592 | tf_op jit(solution)/shard_map/reduce_scatter | solution.py:135
  1060.8 466.1 %reduce-scatter.35.cloned.1.call-start = ((), (), s32[]{:S(2)}) async-start(), calls=%async_computation.23 | async-start | bytes 18874368 | tf_op jit(solution)/shard_map/reduce_scatter | solution.py:135
  1081.6 555.8 %reduce-scatter.33.cloned.1.call-start = ((), (), s32[]{:S(2)}) async-start(), calls=%async_computation.22 | async-start | bytes 18874368 | tf_op jit(solution)/shard_map/reduce_scatter | solution.py:135
  1102.3 645.3 %reduce-scatter.31.cloned.1.call-start = ((), (), s32[]{:S(2)}) async-start(), calls=%async_computation.21 | async-start | bytes 18874368 | tf_op jit(solution)/shard_map/reduce_scatter | solution.py:135
  1119.3 738.9 %reduce-scatter.29.cloned.1.call-start = ((), (), s32[]{:S(2)}) async-start(), calls=%async_computation.20 | async-start | bytes 18874368 | tf_op jit(solution)/shard_map/reduce_scatter | solution.py:135
  (101 other events, 3279.9 us)
Sparse Core Ops, SparseCore 0:
  10.4 25.1 all-gather.40
  38.0 22.4 all-gather.42
  62.9 22.3 all-gather.44
  110.7 21.9 all-gather.46
  135.0 48.9 all-gather.48
  186.3 48.3 all-gather.50
  236.5 22.2 all-gather.54
  260.7 22.2 all-gather.56
  284.6 22.2 all-gather.52
  309.4 48.3 all-gather.60
  360.0 48.3 all-gather.62
  1005.5 46.7 all-reduce.16
  1055.4 41.2 reduce-scatter.26
  1099.9 42.5 reduce-scatter.24
  1145.6 42.4 reduce-scatter.22
  1191.2 42.4 reduce-scatter.20
  1236.8 42.4 reduce-scatter.18
  1282.6 42.4 reduce-scatter.16
  1328.2 42.4 reduce-scatter.14
  1373.9 42.4 reduce-scatter.12
  1419.9 106.9 reduce-scatter.34
  1530.4 106.9 reduce-scatter.32
  1640.7 106.9 reduce-scatter.30
  1751.2 106.9 reduce-scatter.28
  (1 shorter events, 21.9 us)
where the time goes:
time: 1880 us; the launch traced here: 1870 us
  matrix products  906 us (48%)
  waiting for transfers between devices  632 us (34%)
  blocking collectives  176 us (9%)
  other arithmetic  79.3 us (4%)
  local copies, waits for them, and re-layouts  58.3 us (3%)
    reduce_scatter x12, waiting for transfers between devices, step(): lax.psum_scatter(grad_piece, AXIS_NAME, scatter_dimension=0, tiled=True)  628 us
    all_gather x16, blocking collectives, gather(): lax.all_gather(shards[slot][layer_idx], AXIS_NAME, axis=0, tiled=True)  176 us
    dot_general x2, matrix products, layer_backward(): jnp.einsum('bhqs,bqhk->bshk', grad_scores, q_heads, preferred_element_typ...  166 us
    dot_general x2, matrix products, layer_backward(): jnp.einsum('bhqs,bshk->bqhk', grad_scores, k_heads, preferred_element_typ...  166 us
    unnamed x12, matrix products  64.9 us
    sub x2, matrix products, layer_forward(): attn_probs = jax.nn.softmax(jnp.where(causal, scores, -1e+30), axis=-1)  64 us
    dot_general x2, matrix products, layer_backward(): jnp.einsum('bhqs,bqhk->bshk', attn_probs.astype(jnp.bfloat16), grad_mixed...  52.2 us
    dot_general x2, matrix products, layer_backward(): jnp.einsum('td,fd->tf', grad_tok, w_down, preferred_element_type=jnp.floa...  51.6 us
  transfers between devices with their start and end apart: 25, of which 9 were waited for; matrix products, arithmetic and copies ran while one was open for 36% of the time, Pallas kernels for 0%

commit v1 on v0

v1 whole, which is shorter than its diff:
```python
import jax
import jax.numpy as jnp
from jax import lax
from jax.experimental import pallas as pl
from jax.experimental.pallas import tpu as pltpu
from jax.sharding import PartitionSpec as P

ROT = 32
LN_EPS = 1e-5
THETA = 10000.0
AXIS_NAME = 'fsdp'
F32 = jnp.float32
BF16 = jnp.bfloat16
SEQ = 1024
D = 1024
FF = 4096
HEAD = 64
GROUP = 4
GW = GROUP * HEAD
STEPS = 4
QB = 256
VMEM_LIMIT = 60 * 1024 * 1024


def rope_tables(positions):
    half_rot = ROT // 2
    inv_freq = THETA ** (-2.0 * jnp.arange(half_rot, dtype=F32) / ROT)
    angles = positions.astype(F32)[:, None] * inv_freq[None, :]
    cos, sin = jnp.cos(angles), jnp.sin(angles)
    ones = jnp.ones((SEQ, HEAD - ROT), F32)
    zeros = jnp.zeros((SEQ, half_rot), F32)
    wide = jnp.zeros((SEQ, HEAD - ROT), F32)
    keep = jnp.concatenate([cos, cos, ones], axis=1)
    left = jnp.concatenate([-sin, zeros, wide], axis=1)
    right = jnp.concatenate([zeros, sin, wide], axis=1)
    return tuple(jnp.tile(t, (1, GROUP)) for t in (keep, left, right))


def head_mask(head):
    lane = lax.broadcasted_iota(jnp.int32, (1, GW), 1)
    return (lane >= head * HEAD) & (lane < (head + 1) * HEAD)


def causal_mask():
    return lax.broadcasted_iota(jnp.int32, (QB, QB), 0) <= lax.broadcasted_iota(jnp.int32, (QB, QB), 1)


def nt(a, b):
    return lax.dot_general(a, b, (((1,), (1,)), ((), ())), preferred_element_type=F32)


def nn(a, b):
    return lax.dot_general(a, b, (((1,), (0,)), ((), ())), preferred_element_type=F32)


def spin(x, keep, left, right):
    return x * keep + pltpu.roll(x, GW - ROT // 2, 1) * left + pltpu.roll(x, ROT // 2, 1) * right


def unspin(x, keep, left, right):
    return x * keep - pltpu.roll(x, GW - ROT // 2, 1) * left - pltpu.roll(x, ROT // 2, 1) * right


def attn_fwd_kernel(h_ref, w_ref, b_ref, keep_ref, left_ref, right_ref, qkv_ref, mixed_ref, lse_ref):
    h = h_ref[...]
    keep, left, right = keep_ref[...], left_ref[...], right_ref[...]
    q = spin(nn(h, w_ref[:, 0:GW]) + b_ref[:, 0:GW], keep, left, right).astype(BF16)
    qkv_ref[:, 0:GW] = q
    k = spin(nn(h, w_ref[:, GW:2 * GW]) + b_ref[:, GW:2 * GW], keep, left, right).astype(BF16)
    qkv_ref[:, GW:2 * GW] = k
    v = nn(h, w_ref[:, 2 * GW:]) + b_ref[:, 2 * GW:]
    qkv_ref[:, 2 * GW:] = v.astype(BF16)
    v_t = v.T.astype(BF16)
    mask = causal_mask()
    for blk in range(SEQ // QB):
        lo, hi = blk * QB, (blk + 1) * QB
        q_blk = q[lo:hi] * jnp.asarray(HEAD ** -0.5, BF16)
        outs = []
        for head in range(GROUP):
            q_h = jnp.where(head_mask(head), q_blk, jnp.zeros_like(q_blk))
            diag = jnp.where(mask, nt(k[lo:hi], q_h), -1e30)
            top = jnp.max(diag, axis=0, keepdims=True)
            if blk:
                off = nt(k[:lo], q_h)
                top = jnp.maximum(top, jnp.max(off, axis=0, keepdims=True))
            e_diag = jnp.exp(diag - top)
            total = jnp.sum(e_diag, axis=0, keepdims=True)
            if blk:
                e_off = jnp.exp(off - top)
                total = total + jnp.sum(e_off, axis=0, keepdims=True)
            inv = 1.0 / total
            rows = slice(head * HEAD, (head + 1) * HEAD)
            out = nn(v_t[rows, lo:hi], (e_diag * inv).astype(BF16))
            if blk:
                out = out + nn(v_t[rows, :lo], (e_off * inv).astype(BF16))
            outs.append(out)
            lse_ref[0, head:head + 1, lo:hi] = top + jnp.log(total)
        mixed_ref[lo:hi, :] = jnp.concatenate(outs, axis=0).T.astype(BF16)


def attn_fwd(h, w_qkv, b_qkv, tables):
    full = pl.BlockSpec((SEQ, D), lambda i: (0, 0))
    table = pl.BlockSpec((SEQ, GW), lambda i: (0, 0))
    return pl.pallas_call(
        attn_fwd_kernel,
        grid=(STEPS,),
        in_specs=[full, pl.BlockSpec((D, 3 * GW), lambda i: (0, i)), pl.BlockSpec((1, 3 * GW), lambda i: (0, i)), table, table, table],
        out_specs=[pl.BlockSpec((SEQ, 3 * GW), lambda i: (0, i)), pl.BlockSpec((SEQ, GW), lambda i: (0, i)), pl.BlockSpec((1, 8, SEQ), lambda i: (i, 0, 0))],
        out_shape=[jax.ShapeDtypeStruct((SEQ, 3 * D), BF16), jax.ShapeDtypeStruct((SEQ, D), BF16), jax.ShapeDtypeStruct((STEPS, 8, SEQ), F32)],
        compiler_params=pltpu.CompilerParams(vmem_limit_bytes=VMEM_LIMIT),
        cost_estimate=pl.CostEstimate(flops=20_000_000_000, bytes_accessed=20_000_000, transcendentals=10_000_000),
        name='attn_fwd',
    )(h, w_qkv, b_qkv, *tables)


def attn_bwd_kernel(qkv_ref, go_ref, lse_ref, keep_ref, left_ref, right_ref, g_ref, bias_ref, dq_acc, dk_acc, dv_acc):
    q, k, v = qkv_ref[:, 0:GW], qkv_ref[:, GW:2 * GW], qkv_ref[:, 2 * GW:]
    k_t = k.astype(F32).T.astype(BF16)
    dk_acc[...] = jnp.zeros_like(dk_acc)
    dv_acc[...] = jnp.zeros_like(dv_acc)
    mask = causal_mask()
    scale = HEAD ** -0.5
    for blk in range(SEQ // QB):
        lo, hi = blk * QB, (blk + 1) * QB
        q_blk = q[lo:hi]
        go_blk = go_ref[lo:hi, :]
        probs, scores, q_heads, go_heads, dq_t = [], [], [], [], []
        for head in range(GROUP):
            keep_lanes = head_mask(head)
            q_h = jnp.where(keep_lanes, q_blk, jnp.zeros_like(q_blk))
            go_h = jnp.where(keep_lanes, go_blk, jnp.zeros_like(go_blk))
            lse = lse_ref[0, head:head + 1, lo:hi]
            q_s = q_h * jnp.asarray(scale, BF16)
            p = jnp.where(mask, jnp.exp(nt(k[lo:hi], q_s) - lse), 0.0)
            dp = nt(v[lo:hi], go_h)
            delta = jnp.sum(p * dp, axis=0, keepdims=True)
            if blk:
                p_off = jnp.exp(nt(k[:lo], q_s) - lse)
                dp_off = nt(v[:lo], go_h)
                delta = delta + jnp.sum(p_off * dp_off, axis=0, keepdims=True)
            ds = ((p * (dp - delta)) * scale).astype(BF16)
            p = p.astype(BF16)
            if blk:
                ds = jnp.concatenate([((p_off * (dp_off - delta)) * scale).astype(BF16), ds], axis=0)
                p = jnp.concatenate([p_off.astype(BF16), p], axis=0)
            probs.append(p)
            scores.append(ds)
            q_heads.append(q_h)
            go_heads.append(go_h)
            dq_t.append(nn(k_t[head * HEAD:(head + 1) * HEAD, :hi], ds))
        dv_acc[:hi, :] += nn(jnp.concatenate(probs, axis=1), jnp.concatenate(go_heads, axis=0))
        dk_acc[:hi, :] += nn(jnp.concatenate(scores, axis=1), jnp.concatenate(q_heads, axis=0))
        dq_acc[lo:hi, :] = jnp.concatenate(dq_t, axis=0).T
    keep, left, right = keep_ref[...], left_ref[...], right_ref[...]
    sums = []
    for pos, grad in enumerate((unspin(dq_acc[...], keep, left, right), unspin(dk_acc[...], keep, left, right), dv_acc[...])):
        g_ref[:, pos * GW:(pos + 1) * GW] = grad.astype(BF16)
        sums.append(jnp.sum(grad, axis=0, keepdims=True))
    bias_ref[...] = jnp.concatenate([jnp.concatenate(sums, axis=1), jnp.zeros((7, 3 * GW), F32)], axis=0)


def attn_bwd(qkv, grad_mixed, lse, tables):
    wide = pl.BlockSpec((SEQ, 3 * GW), lambda i: (0, i))
    table = pl.BlockSpec((SEQ, GW), lambda i: (0, 0))
    return pl.pallas_call(
        attn_bwd_kernel,
        grid=(STEPS,),
        in_specs=[wide, pl.BlockSpec((SEQ, GW), lambda i: (0, i)), pl.BlockSpec((1, 8, SEQ), lambda i: (i, 0, 0)), table, table, table],
        out_specs=[wide, pl.BlockSpec((8, 3 * GW), lambda i: (0, i))],
        out_shape=[jax.ShapeDtypeStruct((SEQ, 3 * D), BF16), jax.ShapeDtypeStruct((8, 3 * D), F32)],
        scratch_shapes=[pltpu.VMEM((SEQ, GW), F32)] * 3,
        compiler_params=pltpu.CompilerParams(vmem_limit_bytes=VMEM_LIMIT),
        cost_estimate=pl.CostEstimate(flops=50_000_000_000, bytes_accessed=20_000_000, transcendentals=10_000_000),
        name='attn_bwd',
    )(qkv, grad_mixed, lse, *tables)


def wgrad_rows_kernel(core_ref, lhs_ref, lhs2_ref, rhs_ref, rhs2_ref, out_ref):
    out_ref[...] = nn(lhs_ref[...].T, rhs_ref[...]) + nn(lhs2_ref[...].T, rhs2_ref[...])


def wgrad_rows(core, lhs, lhs2, rhs, rhs2):
    tile = 256
    lhs_spec = pl.BlockSpec((SEQ, tile), lambda i, c: (0, (i // 2) * 4 + c[0] * 2 + i % 2))
    rhs_spec = pl.BlockSpec((SEQ, D), lambda i, c: (0, 0))
    return pl.pallas_call(
        wgrad_rows_kernel,
        grid_spec=pltpu.PrefetchScalarGridSpec(
            num_scalar_prefetch=1,
            grid=(FF // 2 // tile,),
            in_specs=[lhs_spec, lhs_spec, rhs_spec, rhs_spec],
            out_specs=pl.BlockSpec((tile, D), lambda i, c: (i, 0)),
        ),
        out_shape=jax.ShapeDtypeStruct((FF // 2, D), F32),
        compiler_params=pltpu.CompilerParams(vmem_limit_bytes=VMEM_LIMIT),
        cost_estimate=pl.CostEstimate(flops=2 * FF * D * SEQ, bytes_accessed=20_000_000, transcendentals=0),
        name='wgrad_rows',
    )(core, lhs, lhs2, rhs, rhs2)


def wgrad_up_kernel(lhs_ref, lhs2_ref, rhs_ref, rhs2_ref, out_ref, left):
    @pl.when(pl.program_id(0) == 0)
    def _():
        left[:, :SEQ] = lhs_ref[...].T
        left[:, SEQ:] = lhs2_ref[...].T

    out_ref[...] = nn(left[:, :SEQ], rhs_ref[...]) + nn(left[:, SEQ:], rhs2_ref[...])


def wgrad_up(lhs, lhs2, rhs, rhs2):
    tile = 512
    lhs_spec = pl.BlockSpec((SEQ, D // 2), lambda i: (0, 0))
    rhs_spec = pl.BlockSpec((SEQ, tile), lambda i: (0, i))
    return pl.pallas_call(
        wgrad_up_kernel,
        grid=(FF // tile,),
        in_specs=[lhs_spec, lhs_spec, rhs_spec, rhs_spec],
        out_specs=pl.BlockSpec((D // 2, tile), lambda i: (0, i)),
        out_shape=jax.ShapeDtypeStruct((D // 2, FF), F32),
        scratch_shapes=[pltpu.VMEM((D // 2, 2 * SEQ), BF16)],
        compiler_params=pltpu.CompilerParams(vmem_limit_bytes=VMEM_LIMIT),
        cost_estimate=pl.CostEstimate(flops=2 * FF * D * SEQ, bytes_accessed=26_000_000, transcendentals=0),
        name='wgrad_up',
    )(lhs, lhs2, rhs, rhs2)


def wgrad_qkvo_kernel(h_ref, h2_ref, mix_ref, mix2_ref, g_ref, g2_ref, tok_ref, tok2_ref, out_ref, left):
    step = pl.program_id(0)

    @pl.when(step == 0)
    def _():
        left[:, :SEQ] = h_ref[...].T
        left[:, SEQ:] = h2_ref[...].T

    @pl.when(step < 6)
    def _():
        out_ref[...] = nn(left[:, :SEQ], g_ref[...]) + nn(left[:, SEQ:], g2_ref[...])

    @pl.when(step == 6)
    def _():
        left[:, :SEQ] = mix_ref[...].T
        left[:, SEQ:] = mix2_ref[...].T

    @pl.when(step >= 6)
    def _():
        out_ref[...] = nn(left[:, :SEQ], tok_ref[...]) + nn(left[:, SEQ:], tok2_ref[...])


def wgrad_qkvo(h, h2, mix, mix2, g, g2, tok, tok2):
    tile = 512
    lhs_spec = pl.BlockSpec((SEQ, D // 2), lambda i: (0, 0))
    g_spec = pl.BlockSpec((SEQ, tile), lambda i: (0, jnp.minimum(i, 5)))
    tok_spec = pl.BlockSpec((SEQ, tile), lambda i: (0, jnp.maximum(i - 6, 0)))
    return pl.pallas_call(
        wgrad_qkvo_kernel,
        grid=(8,),
        in_specs=[lhs_spec] * 4 + [g_spec, g_spec, tok_spec, tok_spec],
        out_specs=pl.BlockSpec((D // 2, tile), lambda i: (0, i)),
        out_shape=jax.ShapeDtypeStruct((D // 2, 4 * D), F32),
        scratch_shapes=[pltpu.VMEM((D // 2, 2 * SEQ), BF16)],
        compiler_params=pltpu.CompilerParams(vmem_limit_bytes=VMEM_LIMIT),
        cost_estimate=pl.CostEstimate(flops=2 * FF * D * SEQ, bytes_accessed=26_000_000, transcendentals=0),
        name='wgrad_qkvo',
    )(h, h2, mix, mix2, g, g2, tok, tok2)


def gelu_tanh(values):
    return jax.nn.gelu(values, approximate=True)


def layer_norm(hidden, gain, bias):
    tok = hidden.astype(F32)
    centred = tok - jnp.mean(tok, axis=-1, keepdims=True)
    inv_std = lax.rsqrt(jnp.mean(centred * centred, axis=-1, keepdims=True) + LN_EPS)
    normed = centred * inv_std
    return normed, inv_std, (normed * gain + bias).astype(BF16)


def interleave(parts):
    return jnp.concatenate([p[:, i * GW:(i + 1) * GW] for i in range(STEPS) for p in parts], axis=1)


def pick_columns(values, core):
    return lax.dynamic_index_in_dim(values.reshape(SEQ, 4, 2, 128), core, 2, keepdims=False).reshape(SEQ, 512)


def solution(mesh):
    group_size = mesh.shape[AXIS_NAME]
    batch_spec = P(AXIS_NAME)
    param_specs = (P(None, AXIS_NAME),) * 14
    swap = [(i, i ^ 1) for i in range(group_size)]
    chips = [[i for i in range(group_size) if i % 2 == c] for c in range(2)]

    def exchange(values):
        return lax.ppermute(values, AXIS_NAME, swap)

    def gather(values):
        return lax.all_gather(values, AXIS_NAME, axis=0, tiled=True)

    def scatter(values):
        return lax.psum_scatter(values, AXIS_NAME, scatter_dimension=0, axis_index_groups=chips, tiled=True)

    def step(hidden, positions, grad_out, *shards):
        (ln_gain, ln_bias, w_query, b_query, w_key, b_key, w_value, b_value, w_out, b_out, w_up, b_up, w_down, b_down) = shards
        layers = ln_gain.shape[0]
        token_total = hidden.shape[0] * hidden.shape[1] * group_size
        rank = lax.axis_index(AXIS_NAME)
        core = lax.rem(rank, 2)
        core_arr = core.reshape(1).astype(jnp.int32)
        tables = rope_tables(positions)

        wide, down = [], []
        for layer in range(layers):
            flat = [w[layer].reshape(w.shape[1], D) for w in (w_query, w_key, w_value)]
            wide.append(gather(jnp.concatenate([interleave(flat), w_up[layer], w_out[layer]], axis=1)))
            down.append(gather(w_down[layer]))

        small = jnp.concatenate([b.reshape(layers, -1) for b in (ln_gain, ln_bias, b_query, b_key, b_value, b_out, b_down, b_up)], axis=1)
        small = gather(small[None])

        current = hidden.reshape(SEQ, D)
        saved = []
        for layer in range(layers):
            mine = small[:, layer]
            (gain, lbias, bq, bk, bv, bo, bd) = [mine[:, i * 128:(i + 1) * 128].reshape(1, D).astype(F32) for i in range(7)]
            bu = mine[:, 7 * 128:].reshape(1, FF).astype(F32)
            weights = wide[layer]
            wqkv, wup, wout, wdown = weights[:, :3 * D], weights[:, 3 * D:3 * D + FF], weights[:, 3 * D + FF:], down[layer]
            normed, inv_std, h = layer_norm(current, gain, lbias)
            up_pre = nn(h, wup) + bu
            act = gelu_tanh(up_pre).astype(BF16)
            qkv, mixed, lse = attn_fwd(h, wqkv, interleave((bq, bk, bv)), tables)
            new = current.astype(F32) + nn(mixed, wout) + bo + nn(act, wdown) + bd
            saved.append((gain, wqkv, wup, wout, wdown, normed, inv_std, h, up_pre, act, qkv, mixed, lse))
            current = new.astype(BF16)

        grad = grad_out.reshape(SEQ, D)
        big, little = [None] * layers, [None] * layers
        for layer in reversed(range(layers)):
            (gain, wqkv, wup, wout, wdown, normed, inv_std, h, up_pre, act, qkv, mixed, lse) = saved[layer]
            grad2 = exchange(grad)
            act2 = exchange(act)
            h2 = exchange(pick_columns(h, 1 - core))
            mixed2 = exchange(pick_columns(mixed, 1 - core))
            h1 = pick_columns(h, core)
            grad_f32 = grad.astype(F32)
            rs_down = scatter(wgrad_rows(core_arr, act, act2, grad, grad2))
            grad_act = nt(grad, wdown).astype(BF16)
            grad_pre = jax.vjp(gelu_tanh, up_pre)[1](grad_act.astype(F32))[0]
            g_b_up = jnp.sum(grad_pre, axis=0)
            grad_pre = grad_pre.astype(BF16)
            rs_up = scatter(wgrad_up(h1, h2, grad_pre, exchange(grad_pre)))
            grad_mixed = nt(grad, wout).astype(BF16)
            g_qkv, g_bias = attn_bwd(qkv, grad_mixed, lse, tables)
            rs_qkvo = scatter(wgrad_qkvo(h1, h2, pick_columns(mixed, core), mixed2, g_qkv, exchange(g_qkv), grad, grad2))
            grad_normed = nt(g_qkv, wqkv) + nt(grad_pre, wup)
            g_gain = jnp.sum(grad_normed * normed, axis=0)
            g_lbias = jnp.sum(grad_normed, axis=0)
            grad_hat = grad_normed * gain
            grad_in = inv_std * (grad_hat - jnp.mean(grad_hat, axis=-1, keepdims=True) - normed * jnp.mean(grad_hat * normed, axis=-1, keepdims=True))
            g_bias = g_bias[0].reshape(STEPS, 3, GW)
            pieces = [g_gain, g_lbias] + [g_bias[:, i].reshape(D) for i in range(3)] + [jnp.sum(grad_f32, axis=0)]
            little[layer] = jnp.concatenate([p.reshape(8, 128) for p in pieces] + [g_b_up.reshape(8, 512)], axis=1)
            big[layer] = (rs_down, rs_up, rs_qkvo)
            grad = (grad_f32 + grad_in).astype(BF16)

        scale = 1.0 / token_total
        everyone = gather(jnp.stack(little, axis=1)[None])
        own = jnp.sum(lax.dynamic_index_in_dim(everyone, rank, 1, keepdims=False), axis=0) * scale
        vec = [own[:, i * 128:(i + 1) * 128] for i in range(6)]

        def stacked(slot, view):
            return jnp.stack([view(big[layer][slot]) * scale for layer in range(layers)])

        def heads(pos):
            def view(rs):
                cols = [rs[:, i * 3 * GW + pos * GW:i * 3 * GW + (pos + 1) * GW] for i in range(STEPS)]
                return jnp.concatenate(cols, axis=1).reshape(-1, 16, HEAD)
            return stacked(2, view)

        return (current.reshape(hidden.shape), grad.reshape(hidden.shape), vec[0], vec[1],
                heads(0), vec[2], heads(1), vec[3], heads(2), vec[4],
                stacked(2, lambda rs: rs[:, 3 * D:]), vec[5],
                stacked(1, lambda rs: rs), own[:, 6 * 128:], stacked(0, lambda rs: rs), vec[5])

    return jax.shard_map(step, mesh=mesh, in_specs=(batch_spec, P(), batch_spec) + param_specs, out_specs=(batch_spec, batch_spec) + param_specs, check_vma=False)
```

time: 1880 us -> 1110 us (0.59)
  matrix products: 906 us -> 197 us
  Pallas kernels: 0 us -> 287 us
  waiting for transfers between devices: 632 us -> 364 us
  blocking collectives: 176 us -> 28.7 us
  local copies, waits for them, and re-layouts: 58.3 us -> 165 us
  other arithmetic: 79.3 us -> 36.6 us
    dot_general x34 -> x14, matrix products: 777 us -> 197 us  [the longest x8 119 us: nt(): lax.dot_general(a, b, (((1,), (1,)), ((), ())), preferred_element_type=F32)]
    reduce_scatter x12 -> x6, waiting for transfers between devices: 628 us -> 203 us  [scatter(): lax.psum_scatter(values, AXIS_NAME, scatter_dimension=0, axis_index_group...]
    pallas_call x0 -> x10, Pallas kernels: none -> 287 us  [the longest x2 96.2 us: attn_bwd(): pl.pallas_call(attn_bwd_kernel, grid=(STEPS,), in_specs=[wide, pl.BlockSp...]
    all_gather x16 -> x2, blocking collectives: 176 us -> 28.7 us  [gather(): return lax.all_gather(values, AXIS_NAME, axis=0, tiled=True)]
    all_gather x12 -> x4, waiting for transfers between devices: 0.07 us -> 109 us  [gather(): return lax.all_gather(values, AXIS_NAME, axis=0, tiled=True)]
    unnamed x12 -> x0, matrix products: 64.9 us -> none
    sub x2 -> x0, matrix products: 64 us -> none  [layer_forward(): attn_probs = jax.nn.softmax(jnp.where(causal, scores, -1e+30), axis=-1)]
    ppermute x0 -> x12, waiting for transfers between devices: none -> 51.5 us  [exchange(): return lax.ppermute(values, AXIS_NAME, swap)]
  transfers between devices with their start and end apart: 25 -> 22, of which waited for: 9 -> 10; matrix products, arithmetic and copies ran while one was open for 36% -> 27% of each run, Pallas kernels for 0% -> 20%
where the time goes in v1:
time: 1110 us; the launch traced here: 1100 us
  waiting for transfers between devices  364 us (33%)
  Pallas kernels  287 us (26%)
  matrix products  197 us (18%)
  local copies, waits for them, and re-layouts  165 us (15%)
  other arithmetic  36.6 us (3%)
  blocking collectives  28.7 us (3%)
  between operations  15.9 us (1%)
    reduce_scatter x6, waiting for transfers between devices, scatter(): lax.psum_scatter(values, AXIS_NAME, scatter_dimension=0, axis_index_group...  203 us
    dot_general x8, matrix products, nt(): lax.dot_general(a, b, (((1,), (1,)), ((), ())), preferred_element_type=F32)  119 us
    all_gather x4, waiting for transfers between devices, gather(): return lax.all_gather(values, AXIS_NAME, axis=0, tiled=True)  109 us
    pallas_call x2, Pallas kernels, attn_bwd(): pl.pallas_call(attn_bwd_kernel, grid=(STEPS,), in_specs=[wide, pl.BlockSp...  96.2 us
    pallas_call x2, Pallas kernels, attn_fwd(): pl.pallas_call(attn_fwd_kernel, grid=(STEPS,), in_specs=[full, pl.BlockSp...  92.2 us
    dot_general x6, matrix products, nn(): lax.dot_general(a, b, (((1,), (0,)), ((), ())), preferred_element_type=F32)  78.1 us
    unnamed x202, local copies, waits for them, and re-layouts  54.4 us
    ppermute x12, waiting for transfers between devices, exchange(): return lax.ppermute(values, AXIS_NAME, swap)  51.5 us
  transfers between devices with their start and end apart: 22, of which 10 were waited for; matrix products, arithmetic and copies ran while one was open for 27% of the time, Pallas kernels for 20%

profile of v1, /device:TPU:0, one launch (start us, length us, event | category | flops | bytes accessed | tf_op | source)
XLA Modules:
  0.0 1097.9 jit_solution(15905976949730434010)
XLA Ops:
  81.0 55.7 %all-gather.10.cloned.1.call-done = bf16[1024,8192]{1,0:T(8,128)(2,1)} async-done(((bf16[128,8192]{1,0:T(8,128)(2,1)}), bf16[1024,8192]{1,0:T(8,128)(2,1)}) %all-gather.10.cloned.1.call-update) | async-done | bytes 16777232 | tf_op jit(solution)/shard_map/all_gather | solution.py:298
  142.7 46.3 %attn_fwd.2 = (bf16[1024,3072]{1,0:T(8,128)(2,1)}, bf16[1024,1024]{1,0:T(8,128)(2,1)}, f32[4,8,1024]{2,1,0:T(8,128)}) custom-call(bf16[1024,1024]{1,0:T(8,128)(2,1)} %add_convert_fusion.1.h_ref, bf16[1024,3072]{1,0:T(8,128)(2,1)} %slice.515.w_ref, f32[1,3072]{1,0:T(1,128)} %copy-done.43, f32[1024,256]{1,0:T(8,128)} %copy.309.keep_ref, ...), custom_call_target="tpu_custom_call" | custom-call | flops 20000000000 | bytes 20000000 | tf_op jit(solution)/shard_map/attn_fwd/pallas_call | solution.py:104
  195.8 18.9 %multiply_convert_fusion.1 = (bf16[1024,4096]{1,0:T(8,128)(2,1)}, f32[1024,4096]{1,0:T(8,128)}) fusion(f32[4096]{0:T(1024)S(1)} %bitcast.254, bf16[1024,1024]{1,0:T(8,128)(2,1)S(1)} %copy-done.11, bf16[1024,8192]{1,0:T(8,128)(2,1)} %all-gather.10.cloned.1.call-done), kind=kOutput, calls=%fused_computation.27 | convolution fusion | flops 8631877632 | bytes 35667968 | tf_op jit(solution)/shard_map/dot_general | solution.py:53
  229.2 44.9 %all-gather.14.cloned.1.call-done = bf16[1,4096,1024]{2,1,0:T(8,128)(2,1)} async-done(((bf16[1,512,1024]{2,1,0:T(8,128)(2,1)}), bf16[1,4096,1024]{2,1,0:T(8,128)(2,1)}) %all-gather.14.cloned.1.call-update) | async-done | bytes 8388624 | tf_op jit(solution)/shard_map/all_gather | solution.py:298
  297.6 45.9 %attn_fwd.3 = (bf16[1024,3072]{1,0:T(8,128)(2,1)}, bf16[1024,1024]{1,0:T(8,128)(2,1)}, f32[4,8,1024]{2,1,0:T(8,128)}) custom-call(bf16[1024,1024]{1,0:T(8,128)(2,1)} %fusion.45.h_ref, bf16[1024,3072]{1,0:T(8,128)(2,1)} %slice.551.w_ref, f32[1,3072]{1,0:T(1,128)} %copy-done.44, f32[1024,256]{1,0:T(8,128)} %copy.309.keep_ref, f32[1024,256]{1,0:T(8,128)} %copy.310.left_ref, ...), custom_call_target="tpu_custom_call" | custom-call | flops 20000000000 | bytes 20000000 | tf_op jit(solution)/shard_map/attn_fwd/pallas_call | solution.py:104
  343.5 48.2 %attn_bwd.2 = (bf16[1024,3072]{1,0:T(8,128)(2,1)}, f32[8,3072]{1,0:T(8,128)}) custom-call(bf16[1024,3072]{1,0:T(8,128)(2,1)} %get-tuple-element.28.qkv_ref, bf16[1024,1024]{1,0:T(8,128)(2,1)} %convert_bitcast_fusion.go_ref, f32[4,8,1024]{2,1,0:T(8,128)} %get-tuple-element.29.lse_ref, f32[1024,256]{1,0:T(8,128)} %copy.309.keep_ref, ...), custom_call_target="tpu_custom_call" | custom-call | flops 49999998976 | bytes 20000000 | tf_op jit(solution)/shard_map/attn_bwd/pallas_call | solution.py:165
  403.9 18.8 %multiply_convert_fusion = (bf16[1024,4096]{1,0:T(8,128)(2,1)}, f32[1024,4096]{1,0:T(8,128)}) fusion(f32[4096]{0:T(1024)S(1)} %bitcast.256, bf16[1024,1024]{1,0:T(8,128)(2,1)S(1)} %copy-done.7, bf16[1024,8192]{1,0:T(8,128)(2,1)} %all-gather.12.cloned.1.call-done), kind=kOutput, calls=%fused_computation.26 | convolution fusion | flops 8631877632 | bytes 35667968 | tf_op jit(solution)/shard_map/dot_general | solution.py:53
  422.7 26.7 %fusion.101 = (f32[4096]{0:T(1024)}, bf16[1024,4096]{1,0:T(8,128)(2,1)}) fusion(f32[1024,4096]{1,0:T(8,128)} %get-tuple-element.159, f32[4096]{0:T(1024)S(1)} %bitcast.257, bf16[1,4096,1024]{2,1,0:T(8,128)(2,1)} %all-gather.16.cloned.1.call-done, bf16[1,1024,1024]{2,1,0:T(8,128)(2,1)} %param.19), kind=kOutput, calls=%fused_computation.256 | convolution fusion | flops 8690593792 | bytes 35684352 | tf_op jit(solution)/shard_map/dot_general | solution.py:49
  449.5 16.6 %fusion.49 = (f32[1024]{0:T(1024)}, f32[1024]{0:T(1024)S(1)}, f32[1024]{0:T(1024)S(1)}, f32[1024]{0:T(1024)}, f32[1024,1024]{1,0:T(8,128)S(1)}) fusion(bf16[1024,1024]{1,0:T(8,128)(2,1)S(1)} %copy-done.3, f32[1024]{0:T(1024)S(1)} %copy-done.25, f32[1024]{0:T(1024)S(1)} %copy-done.21, f32[1024]{0:T(1024)S(1)} %copy-done.27, f32[1024,1024]{1,0:T(8,128)} %fusion.95, ...), kind=kOutput, calls=%fused_computation.62 | convolution fusion | flops 8601464832 | bytes 27291648 | tf_op jit(solution)/shard_map/dot_general | solution.py:49
  475.0 48.0 %attn_bwd.3 = (bf16[1024,3072]{1,0:T(8,128)(2,1)}, f32[8,3072]{1,0:T(8,128)}) custom-call(bf16[1024,3072]{1,0:T(8,128)(2,1)} %get-tuple-element.31.qkv_ref, bf16[1024,1024]{1,0:T(8,128)(2,1)} %convolution_convert_fusion.go_ref, f32[4,8,1024]{2,1,0:T(8,128)} %get-tuple-element.32.lse_ref, f32[1024,256]{1,0:T(8,128)} %copy.309.keep_ref, ...), custom_call_target="tpu_custom_call" | custom-call | flops 49999998976 | bytes 20000000 | tf_op jit(solution)/shard_map/attn_bwd/pallas_call | solution.py:165
  547.2 15.7 %dynamic-slice_reduce_fusion.2 = (bf16[1024,4,128]{2,1,0:T(4,128)(2,1)S(1)}, bf16[1024,4,128]{2,1,0:T(4,128)(2,1)}) fusion(bf16[1024,4,2,128]{3,2,1,0:T(2,128)(2,1)} %reshape.484, s32[]{:T(128)S(6)} %select_n.19, s32[]{:T(128)S(6)} %select_n.18), kind=kLoop, calls=%fused_computation.96 | loop fusion | bytes 4194312 | tf_op jit(solution)/shard_map/jit(dynamic_index_in_dim)/dynamic_slice | solution.py:284
  568.0 18.0 %wgrad_qkvo.2 = f32[512,4096]{1,0:T(8,128)} custom-call(bf16[1024,512]{1,0:T(8,128)(2,1)} %copy.344.h_ref.lhs_ref, bf16[1024,512]{1,0:T(8,128)(2,1)} %collective-permute-done.h2_ref.lhs2_ref, bf16[1024,512]{1,0:T(8,128)(2,1)} %bitcast.230, bf16[1024,512]{1,0:T(8,128)(2,1)} %collective-permute-done.1.mix2_ref, bf16[1024,3072]{1,0:T(8,128)(2,1)} %get-tuple-element.33.g_ref, ...), custom_call_target="tpu_custom_call" | custom-call | flops 8589934592 | bytes 26000000 | tf_op jit(solution)/shard_map/wgrad_qkvo/pallas_call | solution.py:254
  610.5 15.8 %dynamic-slice_reduce_fusion = (bf16[1024,4,128]{2,1,0:T(4,128)(2,1)S(1)}, bf16[1024,4,128]{2,1,0:T(4,128)(2,1)}) fusion(bf16[1024,4,2,128]{3,2,1,0:T(2,128)(2,1)} %reshape.490, s32[]{:T(128)S(6)} %select_n.19, s32[]{:T(128)S(6)} %select_n.18), kind=kLoop, calls=%fused_computation.94 | loop fusion | bytes 4194312 | tf_op jit(solution)/shard_map/jit(dynamic_index_in_dim)/dynamic_slice | solution.py:284
  636.0 18.1 %wgrad_qkvo.3 = f32[512,4096]{1,0:T(8,128)} custom-call(bf16[1024,512]{1,0:T(8,128)(2,1)} %copy.351.h_ref.lhs_ref, bf16[1024,512]{1,0:T(8,128)(2,1)} %collective-permute-done.4.h2_ref.lhs2_ref, bf16[1024,512]{1,0:T(8,128)(2,1)} %bitcast.229, bf16[1024,512]{1,0:T(8,128)(2,1)} %collective-permute-done.5.mix2_ref, bf16[1024,3072]{1,0:T(8,128)(2,1)} %get-tuple-element.30.g_ref, ...), custom_call_target="tpu_custom_call" | custom-call | flops 8589934592 | bytes 26000000 | tf_op jit(solution)/shard_map/wgrad_qkvo/pallas_call | solution.py:254
  667.3 15.0 %wgrad_rows.2 = f32[2048,1024]{1,0:T(8,128)} custom-call(s32[1]{0:T(128)} %bitcast.68.core_ref, bf16[1024,4096]{1,0:T(8,128)(2,1)} %get-tuple-element.154.lhs_ref, bf16[1024,4096]{1,0:T(8,128)(2,1)} %collective-permute-done.10.lhs2_ref, bf16[1024,1024]{1,0:T(8,128)(2,1)} %copy-done.5, bf16[1024,1024]{1,0:T(8,128)(2,1)} %collective-permute-done.3.tok2_ref.rhs2_ref), custom_call_target="tpu_custom_call" | custom-call | flops 8589934592 | bytes 20000000 | tf_op jit(solution)/shard_map/wgrad_rows/pallas_call | solution.py:186
  695.5 15.0 %wgrad_rows.3 = f32[2048,1024]{1,0:T(8,128)} custom-call(s32[1]{0:T(128)} %bitcast.68.core_ref, bf16[1024,4096]{1,0:T(8,128)(2,1)} %get-tuple-element.158.lhs_ref, bf16[1024,4096]{1,0:T(8,128)(2,1)} %collective-permute-done.11.lhs2_ref, bf16[1024,1024]{1,0:T(8,128)(2,1)} %bitcast.228, bf16[1024,1024]{1,0:T(8,128)(2,1)} %collective-permute-done.7.tok2_ref.rhs2_ref), custom_call_target="tpu_custom_call" | custom-call | flops 8589934592 | bytes 20000000 | tf_op jit(solution)/shard_map/wgrad_rows/pallas_call | solution.py:186
  711.2 25.7 %fusion.100 = (f32[4096]{0:T(1024)S(1)}, bf16[1024,4096]{1,0:T(8,128)(2,1)}) fusion(f32[1024,4096]{1,0:T(8,128)} %get-tuple-element.155, f32[4096]{0:T(1024)S(1)} %bitcast.255, bf16[1024,1024]{1,0:T(8,128)(2,1)} %copy-done.5, bf16[1,4096,1024]{2,1,0:T(8,128)(2,1)} %all-gather.14.cloned.1.call-done), kind=kOutput, calls=%fused_computation.255 | convolution fusion | flops 8690593792 | bytes 35684352 | tf_op jit(solution)/shard_map/dot_general | solution.py:49
  750.0 16.3 %wgrad_up.2 = f32[512,4096]{1,0:T(8,128)} custom-call(bf16[1024,512]{1,0:T(8,128)(2,1)} %copy.344.h_ref.lhs_ref, bf16[1024,512]{1,0:T(8,128)(2,1)} %collective-permute-done.h2_ref.lhs2_ref, bf16[1024,4096]{1,0:T(8,128)(2,1)} %get-tuple-element.51.rhs_ref, bf16[1024,4096]{1,0:T(8,128)(2,1)} %collective-permute-done.8.rhs2_ref), custom_call_target="tpu_custom_call" | custom-call | flops 8589934592 | bytes 26000000 | tf_op jit(solution)/shard_map/wgrad_up/pallas_call | solution.py:214
  779.6 16.6 %wgrad_up.3 = f32[512,4096]{1,0:T(8,128)} custom-call(bf16[1024,512]{1,0:T(8,128)(2,1)} %copy.351.h_ref.lhs_ref, bf16[1024,512]{1,0:T(8,128)(2,1)} %collective-permute-done.4.h2_ref.lhs2_ref, bf16[1024,4096]{1,0:T(8,128)(2,1)} %get-tuple-element.53.rhs_ref, bf16[1024,4096]{1,0:T(8,128)(2,1)} %collective-permute-done.9.rhs2_ref), custom_call_target="tpu_custom_call" | custom-call | flops 8589934592 | bytes 26000000 | tf_op jit(solution)/shard_map/wgrad_up/pallas_call | solution.py:214
  808.8 15.1 %multiply_reduce_fusion = (f32[1024]{0:T(1024)S(1)}, f32[1024]{0:T(1024)S(1)}, f32[1024]{0:T(1024)S(1)}, f32[1024]{0:T(1024)S(1)}, f32[1024,1024]{1,0:T(8,128)S(1)}) fusion(bf16[1,1024,1024]{2,1,0:T(8,128)(2,1)S(1)} %copy-done.1, f32[1024]{0:T(1024)S(1)} %copy-done.19, f32[1024]{0:T(1024)S(1)} %copy-done.17, f32[1024]{0:T(1024)S(1)} %copy-done.23, ...), kind=kOutput, calls=%fused_computation.79 | convolution fusion | flops 8601464832 | bytes 27291648 | tf_op jit(solution)/shard_map/dot_general | solution.py:49
  846.9 14.9 %fusion.79 = bf16[1,1024,1024]{2,1,0:T(8,128)(2,1)} fusion(f32[1024]{0:T(1024)S(1)} %copy-done.40, bf16[1024,4096]{1,0:T(8,128)(2,1)} %get-tuple-element.158.lhs_ref, bf16[1,4096,1024]{2,1,0:T(8,128)(2,1)} %all-gather.16.cloned.1.call-done, f32[1024]{0:T(1024)S(1)} %copy-done.41, f32[1024,1024]{1,0:T(8,128)S(1)} %fusion.74, ...), kind=kOutput, calls=%fused_computation.106 | convolution fusion | flops 8596226048 | bytes 25174016 | tf_op jit(solution)/shard_map/dot_general | solution.py:53
  877.2 41.7 %reduce-scatter.17.cloned.1.call-done = f32[512,1024]{1,0:T(8,128)} async-done(((f32[2048,1024]{1,0:T(8,128)}), f32[512,1024]{1,0:T(8,128)}) %reduce-scatter.17.cloned.1.call-update) | async-done | bytes 2097168 | tf_op jit(solution)/shard_map/reduce_scatter | solution.py:301
  923.1 79.5 %reduce-scatter.11.cloned.1.call-done = f32[128,4096]{1,0:T(8,128)} async-done(((f32[512,4096]{1,0:T(8,128)}), f32[128,4096]{1,0:T(8,128)}) %reduce-scatter.11.cloned.1.call-update) | async-done | bytes 2097168 | tf_op jit(solution)/shard_map/reduce_scatter | solution.py:301
  1004.3 81.7 %reduce-scatter.13.cloned.1.call-done = f32[128,4096]{1,0:T(8,128)} async-done(((f32[512,4096]{1,0:T(8,128)}), f32[128,4096]{1,0:T(8,128)}) %reduce-scatter.13.cloned.1.call-update) | async-done | bytes 2097168 | tf_op jit(solution)/shard_map/reduce_scatter | solution.py:301
  (367 shorter events, 322.9 us)
Async XLA Ops:
  7.2 129.6 %all-gather.10.cloned.1.call-start = ((), (), s32[]{:S(2)}) async-start(), calls=%async_computation.6 | async-start | bytes 18874368 | tf_op jit(solution)/shard_map/all_gather | solution.py:298
  49.0 174.3 %all-gather.12.cloned.1.call-start = ((), (), s32[]{:S(2)}) async-start(), calls=%async_computation.7 | async-start | bytes 18874368 | tf_op jit(solution)/shard_map/all_gather | solution.py:298
  50.4 223.7 %all-gather.14.cloned.1.call-start = ((), (), s32[]{:S(2)}) async-start(), calls=%async_computation.14 | async-start | bytes 9437184 | tf_op jit(solution)/shard_map/all_gather | solution.py:298
  53.6 369.1 %all-gather.16.cloned.1.call-start = ((), (), s32[]{:S(2)}) async-start(), calls=%async_computation.15 | async-start | bytes 9437184 | tf_op jit(solution)/shard_map/all_gather | solution.py:298
  54.2 807.6 %reduce-scatter.7.cloned.1.call-start = ((), (), s32[]{:S(2)}) async-start(), calls=%async_computation.8 | async-start | bytes 10485760 | tf_op jit(solution)/shard_map/reduce_scatter | solution.py:301
  70.3 219.3 %copy-start.26 = (f32[1024]{0:T(1024)}, f32[1024]{0:T(1024)S(1)}, u32[]{:S(2)}) copy-start(f32[1024]{0:T(1024)S(1)} %get-tuple-element.138) | copy-start | bytes 12292
  523.0 44.9 %collective-permute-start.2 = (bf16[1024,3072]{1,0:T(8,128)(2,1)}, bf16[1024,3072]{1,0:T(8,128)(2,1)}, u32[]{:S(2)}, u32[]{:S(2)}) collective-permute-start(bf16[1024,3072]{1,0:T(8,128)(2,1)} %get-tuple-element.33.g_ref), channel_id=1, source_target_pairs={{0,1},{1,0},{2,3},{3,2},{4,5},{5,4},{6,7},{7,6}} | collective-permute-start | bytes 18874376 | tf_op jit(solution)/shard_map/ppermute | solution.py:295
  523.3 44.7 %collective-permute-start.3 = (bf16[1024,1024]{1,0:T(8,128)(2,1)}, bf16[1024,1024]{1,0:T(8,128)(2,1)}, u32[]{:S(2)}, u32[]{:S(2)}) collective-permute-start(bf16[1024,1024]{1,0:T(8,128)(2,1)} %copy-done.5), channel_id=1, source_target_pairs={{0,1},{1,0},{2,3},{3,2},{4,5},{5,4},{6,7},{7,6}} | collective-permute-start | bytes 6291464 | tf_op jit(solution)/shard_map/ppermute | solution.py:295
  542.5 25.4 %collective-permute-start = (bf16[1024,512]{1,0:T(8,128)(2,1)}, bf16[1024,512]{1,0:T(8,128)(2,1)}, u32[]{:S(2)}, u32[]{:S(2)}) collective-permute-start(bf16[1024,512]{1,0:T(8,128)(2,1)} %copy.341), channel_id=1, source_target_pairs={{0,1},{1,0},{2,3},{3,2},{4,5},{5,4},{6,7},{7,6}} | collective-permute-start | bytes 3145736 | tf_op jit(solution)/shard_map/ppermute | solution.py:295
  564.0 4.0 collective-permute-start.1
  586.0 277.7 %reduce-scatter.9.cloned.1.call-start = ((), (), s32[]{:S(2)}) async-start(), calls=%async_computation.9 | async-start | bytes 10485760 | tf_op jit(solution)/shard_map/reduce_scatter | solution.py:301
  586.0 49.9 %collective-permute-start.6 = (bf16[1024,3072]{1,0:T(8,128)(2,1)}, bf16[1024,3072]{1,0:T(8,128)(2,1)}, u32[]{:S(2)}, u32[]{:S(2)}) collective-permute-start(bf16[1024,3072]{1,0:T(8,128)(2,1)} %get-tuple-element.30.g_ref), channel_id=1, source_target_pairs={{0,1},{1,0},{2,3},{3,2},{4,5},{5,4},{6,7},{7,6}} | collective-permute-start | bytes 18874376 | tf_op jit(solution)/shard_map/ppermute | solution.py:295
  586.3 49.6 %collective-permute-start.7 = (bf16[1024,1024]{1,0:T(8,128)(2,1)}, bf16[1024,1024]{1,0:T(8,128)(2,1)}, u32[]{:S(2)}, u32[]{:S(2)}) collective-permute-start(bf16[1024,1024]{1,0:T(8,128)(2,1)} %bitcast.226), channel_id=1, source_target_pairs={{0,1},{1,0},{2,3},{3,2},{4,5},{5,4},{6,7},{7,6}} | collective-permute-start | bytes 6291464 | tf_op jit(solution)/shard_map/ppermute | solution.py:295
  605.8 30.1 %collective-permute-start.4 = (bf16[1024,512]{1,0:T(8,128)(2,1)}, bf16[1024,512]{1,0:T(8,128)(2,1)}, u32[]{:S(2)}, u32[]{:S(2)}) collective-permute-start(bf16[1024,512]{1,0:T(8,128)(2,1)} %copy.348), channel_id=1, source_target_pairs={{0,1},{1,0},{2,3},{3,2},{4,5},{5,4},{6,7},{7,6}} | collective-permute-start | bytes 3145736 | tf_op jit(solution)/shard_map/ppermute | solution.py:295
  627.4 8.5 collective-permute-start.5
  654.1 221.3 %reduce-scatter.15.cloned.1.call-start = ((), (), s32[]{:S(2)}) async-start(), calls=%async_computation.12 | async-start | bytes 10485760 | tf_op jit(solution)/shard_map/reduce_scatter | solution.py:301
  654.2 13.1 %collective-permute-start.10 = (bf16[1024,4096]{1,0:T(8,128)(2,1)}, bf16[1024,4096]{1,0:T(8,128)(2,1)}, u32[]{:S(2)}, u32[]{:S(2)}) collective-permute-start(bf16[1024,4096]{1,0:T(8,128)(2,1)} %get-tuple-element.154.lhs_ref), channel_id=1, source_target_pairs={{0,1},{1,0},{2,3},{3,2},{4,5},{5,4},{6,7},{7,6}} | collective-permute-start | bytes 25165832 | tf_op jit(solution)/shard_map/ppermute | solution.py:295
  682.3 236.7 %reduce-scatter.17.cloned.1.call-start = ((), (), s32[]{:S(2)}) async-start(), calls=%async_computation.13 | async-start | bytes 10485760 | tf_op jit(solution)/shard_map/reduce_scatter | solution.py:301
  682.4 13.1 %collective-permute-start.11 = (bf16[1024,4096]{1,0:T(8,128)(2,1)}, bf16[1024,4096]{1,0:T(8,128)(2,1)}, u32[]{:S(2)}, u32[]{:S(2)}) collective-permute-start(bf16[1024,4096]{1,0:T(8,128)(2,1)} %get-tuple-element.158.lhs_ref), channel_id=1, source_target_pairs={{0,1},{1,0},{2,3},{3,2},{4,5},{5,4},{6,7},{7,6}} | collective-permute-start | bytes 25165832 | tf_op jit(solution)/shard_map/ppermute | solution.py:295
  710.5 292.1 %reduce-scatter.11.cloned.1.call-start = ((), (), s32[]{:S(2)}) async-start(), calls=%async_computation.10 | async-start | bytes 10485760 | tf_op jit(solution)/shard_map/reduce_scatter | solution.py:301
  736.9 13.1 %collective-permute-start.8 = (bf16[1024,4096]{1,0:T(8,128)(2,1)}, bf16[1024,4096]{1,0:T(8,128)(2,1)}, u32[]{:S(2)}, u32[]{:S(2)}) collective-permute-start(bf16[1024,4096]{1,0:T(8,128)(2,1)} %get-tuple-element.51.rhs_ref), channel_id=1, source_target_pairs={{0,1},{1,0},{2,3},{3,2},{4,5},{5,4},{6,7},{7,6}} | collective-permute-start | bytes 25165832 | tf_op jit(solution)/shard_map/ppermute | solution.py:295
  766.4 319.6 %reduce-scatter.13.cloned.1.call-start = ((), (), s32[]{:S(2)}) async-start(), calls=%async_computation.11 | async-start | bytes 10485760 | tf_op jit(solution)/shard_map/reduce_scatter | solution.py:301
  766.4 13.1 %collective-permute-start.9 = (bf16[1024,4096]{1,0:T(8,128)(2,1)}, bf16[1024,4096]{1,0:T(8,128)(2,1)}, u32[]{:S(2)}, u32[]{:S(2)}) collective-permute-start(bf16[1024,4096]{1,0:T(8,128)(2,1)} %get-tuple-element.53.rhs_ref), channel_id=1, source_target_pairs={{0,1},{1,0},{2,3},{3,2},{4,5},{5,4},{6,7},{7,6}} | collective-permute-start | bytes 25165832 | tf_op jit(solution)/shard_map/ppermute | solution.py:295
  839.7 250.4 %copy-start.36 = (f32[2,128]{1,0:T(2,128)}, f32[2,128]{1,0:T(2,128)S(1)}, u32[]{:S(2)}) copy-start(f32[2,128]{1,0:T(2,128)S(1)} %get-tuple-element.200) | copy-start | bytes 3076
  (50 other events, 693.5 us)
Sparse Core Ops, SparseCore 0:
  49.1 87.6 all-gather.9
  139.1 84.0 all-gather.11
  225.7 48.3 all-gather.13
  276.3 48.3 all-gather.15
  586.1 80.5 reduce-scatter.6
  669.6 80.5 reduce-scatter.8
  753.1 81.5 reduce-scatter.14
  837.7 81.2 reduce-scatter.16
  922.0 80.5 reduce-scatter.10
  1005.4 80.5 reduce-scatter.12

commit v2 on v1

v2 whole, which is shorter than its diff:
```python
import functools

import jax
import jax.numpy as jnp
from jax import lax
from jax.experimental import pallas as pl
from jax.experimental.pallas import tpu as pltpu
from jax.sharding import PartitionSpec as P

ROT = 32
LN_EPS = 1e-5
THETA = 10000.0
AXIS_NAME = 'fsdp'
F32 = jnp.float32
BF16 = jnp.bfloat16
SEQ = 1024
D = 1024
FF = 4096
HEAD = 64
GROUP = 4
GW = GROUP * HEAD
STEPS = 4
QB = 256
VMEM_LIMIT = 60 * 1024 * 1024


def rope_tables(positions):
    half_rot = ROT // 2
    inv_freq = THETA ** (-2.0 * jnp.arange(half_rot, dtype=F32) / ROT)
    angles = positions.astype(F32)[:, None] * inv_freq[None, :]
    cos, sin = jnp.cos(angles), jnp.sin(angles)
    ones = jnp.ones((SEQ, HEAD - ROT), F32)
    zeros = jnp.zeros((SEQ, half_rot), F32)
    wide = jnp.zeros((SEQ, HEAD - ROT), F32)
    keep = jnp.concatenate([cos, cos, ones], axis=1)
    left = jnp.concatenate([-sin, zeros, wide], axis=1)
    right = jnp.concatenate([zeros, sin, wide], axis=1)
    return tuple(jnp.tile(t, (1, GROUP)) for t in (keep, left, right))


def head_mask(head):
    lane = lax.broadcasted_iota(jnp.int32, (1, GW), 1)
    return (lane >= head * HEAD) & (lane < (head + 1) * HEAD)


def causal_mask():
    return lax.broadcasted_iota(jnp.int32, (QB, QB), 0) <= lax.broadcasted_iota(jnp.int32, (QB, QB), 1)


def nt(a, b):
    return lax.dot_general(a, b, (((1,), (1,)), ((), ())), preferred_element_type=F32)


def nn(a, b):
    return lax.dot_general(a, b, (((1,), (0,)), ((), ())), preferred_element_type=F32)


def spin(x, keep, left, right):
    return x * keep + pltpu.roll(x, GW - ROT // 2, 1) * left + pltpu.roll(x, ROT // 2, 1) * right


def unspin(x, keep, left, right):
    return x * keep - pltpu.roll(x, GW - ROT // 2, 1) * left - pltpu.roll(x, ROT // 2, 1) * right


def attn_fwd_kernel(h_ref, wq_ref, wk_ref, wv_ref, bq_ref, bk_ref, bv_ref, keep_ref, left_ref, right_ref, qkv_ref, mixed_ref, lse_ref):
    h = h_ref[...]
    keep, left, right = keep_ref[...], left_ref[...], right_ref[...]
    q = spin(nn(h, wq_ref[...]) + bq_ref[...], keep, left, right).astype(BF16)
    qkv_ref[0] = q
    k = spin(nn(h, wk_ref[...]) + bk_ref[...], keep, left, right).astype(BF16)
    qkv_ref[1] = k
    v = nn(h, wv_ref[...]) + bv_ref[...]
    qkv_ref[2] = v.astype(BF16)
    v_t = v.T.astype(BF16)
    mask = causal_mask()
    for blk in range(SEQ // QB):
        lo, hi = blk * QB, (blk + 1) * QB
        q_blk = q[lo:hi] * jnp.asarray(HEAD ** -0.5, BF16)
        outs = []
        for head in range(GROUP):
            q_h = jnp.where(head_mask(head), q_blk, jnp.zeros_like(q_blk))
            diag = jnp.where(mask, nt(k[lo:hi], q_h), -1e30)
            top = jnp.max(diag, axis=0, keepdims=True)
            if blk:
                off = nt(k[:lo], q_h)
                top = jnp.maximum(top, jnp.max(off, axis=0, keepdims=True))
            e_diag = jnp.exp(diag - top)
            total = jnp.sum(e_diag, axis=0, keepdims=True)
            if blk:
                e_off = jnp.exp(off - top)
                total = total + jnp.sum(e_off, axis=0, keepdims=True)
            inv = 1.0 / total
            rows = slice(head * HEAD, (head + 1) * HEAD)
            out = nn(v_t[rows, lo:hi], (e_diag * inv).astype(BF16))
            if blk:
                out = out + nn(v_t[rows, :lo], (e_off * inv).astype(BF16))
            outs.append(out)
            lse_ref[0, head:head + 1, lo:hi] = top + jnp.log(total)
        mixed_ref[lo:hi, :] = jnp.concatenate(outs, axis=0).T.astype(BF16)


def attn_fwd(h, weights, biases, tables):
    full = pl.BlockSpec((SEQ, D), lambda i: (0, 0))
    table = pl.BlockSpec((SEQ, GW), lambda i: (0, 0))
    w_specs = [pl.BlockSpec((D, GW), lambda i, pos=pos: (0, pos * STEPS + i)) for pos in range(3)]
    b_spec = pl.BlockSpec((1, GW), lambda i: (0, i))
    return pl.pallas_call(
        attn_fwd_kernel,
        grid=(STEPS,),
        in_specs=[full] + w_specs + [b_spec] * 3 + [table] * 3,
        out_specs=[pl.BlockSpec((3, SEQ, GW), lambda i: (0, 0, i)), pl.BlockSpec((SEQ, GW), lambda i: (0, i)), pl.BlockSpec((1, 8, SEQ), lambda i: (i, 0, 0))],
        out_shape=[jax.ShapeDtypeStruct((3, SEQ, D), BF16), jax.ShapeDtypeStruct((SEQ, D), BF16), jax.ShapeDtypeStruct((STEPS, 8, SEQ), F32)],
        compiler_params=pltpu.CompilerParams(vmem_limit_bytes=VMEM_LIMIT),
        cost_estimate=pl.CostEstimate(flops=20_000_000_000, bytes_accessed=20_000_000, transcendentals=10_000_000),
        name='attn_fwd',
    )(h, weights, weights, weights, *biases, *tables)


def attn_bwd_kernel(qkv_ref, go_ref, lse_ref, keep_ref, left_ref, right_ref, g_ref, bias_ref, dq_acc, dk_acc, dv_acc):
    q, k, v = qkv_ref[0], qkv_ref[1], qkv_ref[2]
    k_t = k.astype(F32).T.astype(BF16)
    dk_acc[...] = jnp.zeros_like(dk_acc)
    dv_acc[...] = jnp.zeros_like(dv_acc)
    mask = causal_mask()
    scale = HEAD ** -0.5
    for blk in range(SEQ // QB):
        lo, hi = blk * QB, (blk + 1) * QB
        q_blk = q[lo:hi]
        go_blk = go_ref[lo:hi, :]
        probs, scores, q_heads, go_heads, dq_t = [], [], [], [], []
        for head in range(GROUP):
            keep_lanes = head_mask(head)
            q_h = jnp.where(keep_lanes, q_blk, jnp.zeros_like(q_blk))
            go_h = jnp.where(keep_lanes, go_blk, jnp.zeros_like(go_blk))
            lse = lse_ref[0, head:head + 1, lo:hi]
            q_s = q_h * jnp.asarray(scale, BF16)
            p = jnp.where(mask, jnp.exp(nt(k[lo:hi], q_s) - lse), 0.0)
            dp = nt(v[lo:hi], go_h)
            delta = jnp.sum(p * dp, axis=0, keepdims=True)
            if blk:
                p_off = jnp.exp(nt(k[:lo], q_s) - lse)
                dp_off = nt(v[:lo], go_h)
                delta = delta + jnp.sum(p_off * dp_off, axis=0, keepdims=True)
            ds = ((p * (dp - delta)) * scale).astype(BF16)
            p = p.astype(BF16)
            if blk:
                ds = jnp.concatenate([((p_off * (dp_off - delta)) * scale).astype(BF16), ds], axis=0)
                p = jnp.concatenate([p_off.astype(BF16), p], axis=0)
            probs.append(p)
            scores.append(ds)
            q_heads.append(q_h)
            go_heads.append(go_h)
            dq_t.append(nn(k_t[head * HEAD:(head + 1) * HEAD, :hi], ds))
        dv_acc[:hi, :] += nn(jnp.concatenate(probs, axis=1), jnp.concatenate(go_heads, axis=0))
        dk_acc[:hi, :] += nn(jnp.concatenate(scores, axis=1), jnp.concatenate(q_heads, axis=0))
        dq_acc[lo:hi, :] = jnp.concatenate(dq_t, axis=0).T
    keep, left, right = keep_ref[...], left_ref[...], right_ref[...]
    sums = []
    for pos, grad in enumerate((unspin(dq_acc[...], keep, left, right), unspin(dk_acc[...], keep, left, right), dv_acc[...])):
        g_ref[pos] = grad.astype(BF16)
        sums.append(jnp.sum(grad, axis=0, keepdims=True))
    bias_ref[...] = jnp.concatenate([jnp.concatenate(sums, axis=1), jnp.zeros((7, 3 * GW), F32)], axis=0)


def attn_bwd(qkv, grad_mixed, lse, tables):
    wide = pl.BlockSpec((3, SEQ, GW), lambda i: (0, 0, i))
    table = pl.BlockSpec((SEQ, GW), lambda i: (0, 0))
    return pl.pallas_call(
        attn_bwd_kernel,
        grid=(STEPS,),
        in_specs=[wide, pl.BlockSpec((SEQ, GW), lambda i: (0, i)), pl.BlockSpec((1, 8, SEQ), lambda i: (i, 0, 0)), table, table, table],
        out_specs=[wide, pl.BlockSpec((8, 3 * GW), lambda i: (0, i))],
        out_shape=[jax.ShapeDtypeStruct((3, SEQ, D), BF16), jax.ShapeDtypeStruct((8, 3 * D), F32)],
        scratch_shapes=[pltpu.VMEM((SEQ, GW), F32)] * 3,
        compiler_params=pltpu.CompilerParams(vmem_limit_bytes=VMEM_LIMIT),
        cost_estimate=pl.CostEstimate(flops=50_000_000_000, bytes_accessed=20_000_000, transcendentals=10_000_000),
        name='attn_bwd',
    )(qkv, grad_mixed, lse, *tables)


def wgrad_rows_kernel(core_ref, lhs_ref, lhs2_ref, rhs_ref, rhs2_ref, out_ref):
    out_ref[...] = nn(lhs_ref[...].T, rhs_ref[...]) + nn(lhs2_ref[...].T, rhs2_ref[...])


def wgrad_rows(core, lhs, lhs2, rhs, rhs2):
    tile = 256
    lhs_spec = pl.BlockSpec((SEQ, tile), lambda i, c: (0, (i // 2) * 4 + c[0] * 2 + i % 2))
    rhs_spec = pl.BlockSpec((SEQ, D), lambda i, c: (0, 0))
    return pl.pallas_call(
        wgrad_rows_kernel,
        grid_spec=pltpu.PrefetchScalarGridSpec(
            num_scalar_prefetch=1,
            grid=(FF // 2 // tile,),
            in_specs=[lhs_spec, lhs_spec, rhs_spec, rhs_spec],
            out_specs=pl.BlockSpec((tile, D), lambda i, c: (i, 0)),
        ),
        out_shape=jax.ShapeDtypeStruct((FF // 2, D), F32),
        compiler_params=pltpu.CompilerParams(vmem_limit_bytes=VMEM_LIMIT),
        cost_estimate=pl.CostEstimate(flops=2 * FF * D * SEQ, bytes_accessed=20_000_000, transcendentals=0),
        name='wgrad_rows',
    )(core, lhs, lhs2, rhs, rhs2)


TILE = 512


def segment_tiles(rhs):
    return rhs.size // (SEQ * TILE)


def wgrad_cols_kernel(plan, *refs):
    lefts = sorted({p[0] for p in plan}, reverse=False)
    n_left = 8 * len(lefts)
    rhs_refs = refs[1 + n_left:1 + n_left + 2 * len(plan)]
    out_ref, left = refs[-2], refs[-1]
    step = pl.program_id(0)
    loaded = None
    for seg, (which, first, last) in enumerate(plan):
        if which != loaded:
            blocks = refs[1 + 8 * lefts.index(which):1 + 8 * lefts.index(which) + 8]
            loaded = which

            @pl.when(step == first)
            def _(blocks=blocks):
                for j in range(4):
                    left[128 * j:128 * (j + 1), :SEQ] = blocks[j][...].T
                    left[128 * j:128 * (j + 1), SEQ:] = blocks[4 + j][...].T

        here, there = rhs_refs[2 * seg], rhs_refs[2 * seg + 1]

        @pl.when((step >= first) & (step < last))
        def _(here=here, there=there):
            a, b = (here[0], there[0]) if len(here.shape) == 3 else (here[...], there[...])
            out_ref[...] = nn(left[:, :SEQ], a) + nn(left[:, SEQ:], b)


def wgrad_cols(core, lefts, segments):
    plan, specs, args, first = [], [], [], 0
    for mine, partner in lefts:
        for values in (mine, partner):
            for j in range(4):
                specs.append(pl.BlockSpec((SEQ, 128), lambda i, c, j=j: (0, 2 * j + c[0])))
                args.append(values)
    for which, mine, partner in segments:
        tiles = segment_tiles(mine)

        def place(i, c, first=first, tiles=tiles, deep=mine.ndim == 3):
            pos = jnp.clip(i - first, 0, tiles - 1)
            return (pos // 2, 0, pos % 2) if deep else (0, pos)

        shape = (1, SEQ, TILE) if mine.ndim == 3 else (SEQ, TILE)
        specs += [pl.BlockSpec(shape, place)] * 2
        args += [mine, partner]
        plan.append((which, first, first + tiles))
        first += tiles
    return pl.pallas_call(
        functools.partial(wgrad_cols_kernel, tuple(plan)),
        grid_spec=pltpu.PrefetchScalarGridSpec(
            num_scalar_prefetch=1,
            grid=(first,),
            in_specs=specs,
            out_specs=pl.BlockSpec((D // 2, TILE), lambda i, c: (0, i)),
            scratch_shapes=[pltpu.VMEM((D // 2, 2 * SEQ), BF16)],
        ),
        out_shape=jax.ShapeDtypeStruct((D // 2, first * TILE), F32),
        compiler_params=pltpu.CompilerParams(vmem_limit_bytes=VMEM_LIMIT),
        cost_estimate=pl.CostEstimate(flops=2 * SEQ * D * first * TILE, bytes_accessed=3_200_000 * first, transcendentals=0),
        name='wgrad_cols',
    )(core, *args)


def gelu_tanh(values):
    return jax.nn.gelu(values, approximate=True)


def layer_norm(hidden, gain, bias):
    tok = hidden.astype(F32)
    centred = tok - jnp.mean(tok, axis=-1, keepdims=True)
    inv_std = lax.rsqrt(jnp.mean(centred * centred, axis=-1, keepdims=True) + LN_EPS)
    normed = centred * inv_std
    return normed, inv_std, (normed * gain + bias).astype(BF16)


def bar(*values):
    return lax.optimization_barrier(values)


def solution(mesh):
    group_size = mesh.shape[AXIS_NAME]
    batch_spec = P(AXIS_NAME)
    param_specs = (P(None, AXIS_NAME),) * 14
    swap = [(i, i ^ 1) for i in range(group_size)]
    chips = [[i for i in range(group_size) if i % 2 == c] for c in range(2)]

    def exchange(values):
        return lax.ppermute(values, AXIS_NAME, swap)

    def gather(values):
        return lax.all_gather(values, AXIS_NAME, axis=0, tiled=True)

    def scatter(values):
        return lax.psum_scatter(values, AXIS_NAME, scatter_dimension=0, axis_index_groups=chips, tiled=True)

    def step(hidden, positions, grad_out, *shards):
        (ln_gain, ln_bias, w_query, b_query, w_key, b_key, w_value, b_value, w_out, b_out, w_up, b_up, w_down, b_down) = shards
        layers = ln_gain.shape[0]
        token_total = hidden.shape[0] * hidden.shape[1] * group_size
        rank = lax.axis_index(AXIS_NAME)
        core = lax.rem(rank, 2)
        core_arr = core.reshape(1).astype(jnp.int32)
        tables = rope_tables(positions)

        wide, down = [], []
        sources = (w_query, w_key, w_value, w_up, w_out)
        for layer in range(layers):
            joined = jnp.concatenate([w[layer].reshape(w.shape[1], -1) for w in sources], axis=1)
            if layer == 0:
                joined, *sources = bar(joined, *sources)
            wide.append(gather(joined))
            down.append(gather(w_down[layer]))

        small = jnp.concatenate([b.reshape(layers, -1) for b in (ln_gain, ln_bias, b_query, b_key, b_value, b_out, b_down, b_up)], axis=1)
        small = gather(small[None])

        def split(layer):
            mine = small[:, layer]
            vecs = [mine[:, i * 128:(i + 1) * 128].reshape(1, D).astype(F32) for i in range(7)]
            return vecs + [mine[:, 7 * 128:].reshape(1, FF).astype(F32)]

        def mlp_up(h, wup, bu):
            up_pre = nn(h, wup) + bu
            return up_pre, gelu_tanh(up_pre).astype(BF16)

        def finish(current, mixed, wout, bo, act, wdown, bd):
            return (current.astype(F32) + nn(mixed, wout) + bo + nn(act, wdown) + bd).astype(BF16)

        def mlp_pull(grad, wdown, up_pre):
            grad_act = nt(grad, wdown).astype(BF16)
            grad_pre = jax.vjp(gelu_tanh, up_pre)[1](grad_act.astype(F32))[0]
            return grad_pre.astype(BF16), jnp.sum(grad_pre, axis=0)

        def norm_pull(grad, grad_normed, normed, inv_std, gain):
            grad_hat = grad_normed * gain
            grad_in = inv_std * (grad_hat - jnp.mean(grad_hat, axis=-1, keepdims=True) - normed * jnp.mean(grad_hat * normed, axis=-1, keepdims=True))
            return (grad.astype(F32) + grad_in).astype(BF16), jnp.sum(grad_normed * normed, axis=0), jnp.sum(grad_normed, axis=0)

        def back_qkv(g, weights):
            return sum(nt(g[pos], weights[:, pos * D:(pos + 1) * D]) for pos in range(3))

        def pack(g_gain, g_lbias, g_bias, grad, g_b_up):
            g_bias = g_bias[0].reshape(STEPS, 3, GW)
            pieces = [g_gain, g_lbias] + [g_bias[:, i].reshape(D) for i in range(3)] + [jnp.sum(grad.astype(F32), axis=0)]
            return jnp.concatenate([p.reshape(8, 128) for p in pieces] + [g_b_up.reshape(8, 512)], axis=1)

        up_cols, out_cols = slice(3 * D, 3 * D + FF), slice(3 * D + FF, None)

        x0 = hidden.reshape(SEQ, D)
        gain0, lbias0, bq, bk, bv, bo, bd, bu = split(0)
        normed0, inv0, h0 = layer_norm(x0, gain0, lbias0)
        qkv0, mixed0, lse0 = attn_fwd(h0, wide[0], (bq, bk, bv), tables)
        up_pre0, act0 = mlp_up(h0, wide[0][:, up_cols], bu)
        x1 = finish(x0, mixed0, wide[0][:, out_cols], bo, act0, down[0], bd)
        h0x, act0x, mixed0x = exchange(h0), exchange(act0), exchange(mixed0)

        top = grad_out.reshape(SEQ, D)
        topx = exchange(top)
        gain1, lbias1, bq, bk, bv, bo1, bd1, bu = split(1)
        normed1, inv1, h1 = layer_norm(x1, gain1, lbias1)
        up_pre1, act1 = mlp_up(h1, wide[1][:, up_cols], bu)
        h1x, act1x = exchange(h1), exchange(act1)
        dw, top_a = bar(wgrad_rows(core_arr, act1, act1x, top, topx), top)
        rs_down1 = scatter(dw)
        pre1, g_bup1 = mlp_pull(top_a, down[1], up_pre1)
        pre1x = exchange(pre1)
        pre1_a, h1_a = bar(pre1, h1)
        qkv1, mixed1, lse1 = attn_fwd(h1_a, wide[1], (bq, bk, bv), tables)
        mixed1x = exchange(mixed1)
        mixed1_a, pre1_b = bar(mixed1, pre1_a)
        dw, top_b = bar(wgrad_cols(core_arr, [(h1, h1x)], [(0, pre1_b, pre1x)]), top_a)
        rs_up1 = scatter(dw)
        g1, g_bias1 = attn_bwd(qkv1, nt(top_b, wide[1][:, out_cols]).astype(BF16), lse1, tables)
        g1x = exchange(g1)
        g1_a, pre1_c = bar(g1, pre1_b)
        back1 = nt(pre1_c, wide[1][:, up_cols])
        g1_b, back1 = bar(g1_a, back1)
        dw, g1_c = bar(wgrad_cols(core_arr, [(h1, h1x), (mixed1_a, mixed1x)], [(0, g1_b, g1x), (1, top, topx)]), g1_b)
        rs_qkvo1 = scatter(dw)
        mid, g_gain, g_lbias = norm_pull(top, back1 + back_qkv(g1_c, wide[1]), normed1, inv1, gain1)
        little1 = pack(g_gain, g_lbias, g_bias1, top, g_bup1)

        midx = exchange(mid)
        pre0, g_bup0 = mlp_pull(mid, down[0], up_pre0)
        pre0x = exchange(pre0)
        pre0_a, mid_a = bar(pre0, mid)
        dw, mid_b = bar(wgrad_rows(core_arr, act0, act0x, mid_a, midx), mid_a)
        rs_down0 = scatter(dw)
        g0, g_bias0 = attn_bwd(qkv0, nt(mid_b, wide[0][:, out_cols]).astype(BF16), lse0, tables)
        g0x = exchange(g0)
        g0_a, pre0_b = bar(g0, pre0_a)
        back0 = nt(pre0_b, wide[0][:, up_cols])
        g0_b, back0 = bar(g0_a, back0)
        dw = wgrad_cols(core_arr, [(h0, h0x), (mixed0, mixed0x)], [(0, g0_b, g0x), (0, pre0_b, pre0x), (1, mid_b, midx)])
        dw, g0_c, mixed1_b, act1_b = bar(dw, g0_b, mixed1_a, act1)
        rs_wide0 = scatter(dw)
        grad, g_gain, g_lbias = norm_pull(mid, back0 + back_qkv(g0_c, wide[0]), normed0, inv0, gain0)
        little0 = pack(g_gain, g_lbias, g_bias0, mid, g_bup0)
        current = finish(x1, mixed1_b, wide[1][:, out_cols], bo1, act1_b, down[1], bd1)
        little = [little0, little1]

        scale = 1.0 / token_total
        everyone = gather(jnp.stack(little, axis=1)[None])
        own = jnp.sum(lax.dynamic_index_in_dim(everyone, rank, 1, keepdims=False), axis=0) * scale
        vec = [own[:, i * 128:(i + 1) * 128] for i in range(6)]

        def stacked(first, second):
            return jnp.stack([first * scale, second * scale])

        def heads(pos):
            cols = slice(pos * D, (pos + 1) * D)
            return stacked(rs_wide0[:, cols].reshape(-1, 16, HEAD), rs_qkvo1[:, cols].reshape(-1, 16, HEAD))

        return (current.reshape(hidden.shape), grad.reshape(hidden.shape), vec[0], vec[1],
                heads(0), vec[2], heads(1), vec[3], heads(2), vec[4],
                stacked(rs_wide0[:, out_cols], rs_qkvo1[:, 3 * D:]), vec[5],
                stacked(rs_wide0[:, up_cols], rs_up1), own[:, 6 * 128:], stacked(rs_down0, rs_down1), vec[5])

    return jax.shard_map(step, mesh=mesh, in_specs=(batch_spec, P(), batch_spec) + param_specs, out_specs=(batch_spec, batch_spec) + param_specs, check_vma=False)
```

time: 1110 us -> 828 us (0.75)
  waiting for transfers between devices: 364 us -> 197 us
  local copies, waits for them, and re-layouts: 165 us -> 41.1 us
    reduce_scatter x6 -> x5, waiting for transfers between devices: 203 us -> 76.4 us  [scatter(): lax.psum_scatter(values, AXIS_NAME, scatter_dimension=0, axis_index_group...]
    dynamic_slice x4 -> x0, local copies, waits for them, and re-layouts: 41.2 us -> none  [pick_columns(): lax.dynamic_index_in_dim(values.reshape(SEQ, 4, 2, 128), core, 2, keepdim...]
    unnamed x202 -> x150, local copies, waits for them, and re-layouts: 54.4 us -> 15 us
    ppermute x12, waiting for transfers between devices: 51.5 us -> 20.5 us  [exchange(): return lax.ppermute(values, AXIS_NAME, swap)]
    reshape x9 -> x2, local copies, waits for them, and re-layouts: 20.1 us -> 0.01 us  [pack(): g_b_up.reshape(8, 512)]
    slice x18 -> x14, local copies, waits for them, and re-layouts: 24.3 us -> 4.96 us  [the longest x9 2.98 us: step(): w[layer].reshape(w.shape[1], -1)]
    convert_element_type x4 -> x0, local copies, waits for them, and re-layouts: 12.4 us -> none  [the longest x2 12.4 us: step(): new = current.astype(F32) + nn(mixed, wout) + bo + nn(act, wdown) + bd]
    dot_general x8 -> x12, matrix products: 119 us -> 130 us  [nt(): lax.dot_general(a, b, (((1,), (1,)), ((), ())), preferred_element_type=F32)]
  transfers between devices with their start and end apart: 22 -> 21, of which waited for: 10 -> 4; matrix products, arithmetic and copies ran while one was open for 27% -> 31% of each run, Pallas kernels for 20% -> 35%
where the time goes in v2:
time: 828 us; the launch traced here: 821 us
  Pallas kernels  288 us (35%)
  matrix products  206 us (25%)
  waiting for transfers between devices  197 us (24%)
  local copies, waits for them, and re-layouts  41.1 us (5%)
  other arithmetic  37.3 us (5%)
  blocking collectives  33.2 us (4%)
  between operations  15.3 us (2%)
    dot_general x12, matrix products, nt(): lax.dot_general(a, b, (((1,), (1,)), ((), ())), preferred_element_type=F32)  130 us
    all_gather x4, waiting for transfers between devices, gather(): return lax.all_gather(values, AXIS_NAME, axis=0, tiled=True)  99.5 us
    pallas_call x2, Pallas kernels, attn_bwd(): pl.pallas_call(attn_bwd_kernel, grid=(STEPS,), in_specs=[wide, pl.BlockSp...  96.6 us
    pallas_call x2, Pallas kernels, attn_fwd(): pl.pallas_call(attn_fwd_kernel, grid=(STEPS,), in_specs=[full] + w_specs...  92.9 us
    reduce_scatter x5, waiting for transfers between devices, scatter(): lax.psum_scatter(values, AXIS_NAME, scatter_dimension=0, axis_index_group...  76.4 us
    dot_general x6, matrix products, nn(): lax.dot_general(a, b, (((1,), (0,)), ((), ())), preferred_element_type=F32)  75.9 us
    pallas_call x3, Pallas kernels, wgrad_cols(): pl.pallas_call(functools.partial(wgrad_cols_kernel, tuple(plan)), grid_sp...  68.4 us
    all_gather x2, blocking collectives, gather(): return lax.all_gather(values, AXIS_NAME, axis=0, tiled=True)  33.2 us
  transfers between devices with their start and end apart: 21, of which 4 were waited for; matrix products, arithmetic and copies ran while one was open for 31% of the time, Pallas kernels for 35%

profile of v2, /device:TPU:0, one launch (start us, length us, event | category | flops | bytes accessed | tf_op | source)
XLA Modules:
  0.0 821.4 jit_solution(18425642972489348551)
XLA Ops:
  24.5 14.6 %all-gather.4 = bf16[8,2,1408]{2,1,0:T(2,128)(2,1)S(1)} all-gather(bf16[1,2,1408]{2,1,0:T(2,128)(2,1)S(1)} %bitcast.260), channel_id=2, replica_groups=mesh['fsdp'=8] {'fsdp'}, dimensions={0}, use_global_device_ids=true | all-gather | bytes 50688 | tf_op jit(solution)/shard_map/all_gather | solution.py:300
  50.2 50.6 %all-gather.10.cloned.1.call-done.wq_ref.wk_ref.wv_ref = bf16[1024,8192]{1,0:T(8,128)(2,1)} async-done(((bf16[128,8192]{1,0:T(8,128)(2,1)}), bf16[1024,8192]{1,0:T(8,128)(2,1)}) %all-gather.10.cloned.1.call-update) | async-done | bytes 16777232 | tf_op jit(solution)/shard_map/all_gather | solution.py:300
  100.8 46.3 %attn_fwd.2 = (bf16[3,1024,1024]{2,1,0:T(8,128)(2,1)}, bf16[1024,1024]{1,0:T(8,128)(2,1)}, f32[4,8,1024]{2,1,0:T(8,128)}) custom-call(bf16[1024,1024]{1,0:T(8,128)(2,1)} %fusion.60.h_ref.refs_1_.refs_2_.refs_3_.refs_4_, bf16[1024,8192]{1,0:T(8,128)(2,1)} %all-gather.10.cloned.1.call-done.wq_ref.wk_ref.wv_ref, ...), custom_call_target="tpu_custom_call" | custom-call | flops 20000000000 | bytes 20000000 | tf_op jit(solution)/shard_map/attn_fwd/pallas_call | solution.py:108
  153.9 19.0 %multiply_convert_fusion.1 = (bf16[1024,4096]{1,0:T(8,128)(2,1)}, f32[1024,4096]{1,0:T(8,128)}) fusion(f32[4096]{0:T(1024)S(1)} %bitcast.250, bf16[1024,1024]{1,0:T(8,128)(2,1)S(1)} %copy-done.1, bf16[1024,8192]{1,0:T(8,128)(2,1)} %all-gather.10.cloned.1.call-done.wq_ref.wk_ref.wv_ref), kind=kOutput, calls=%fused_computation.27 | convolution fusion | flops 8631877632 | bytes 35667968 | tf_op jit(solution)/shard_map/dot_general | solution.py:55
  172.8 14.6 %convert_reduce_fusion = (f32[1024]{0:T(1024)S(1)}, bf16[1024,1024]{1,0:T(8,128)(2,1)S(1)}) fusion(f32[1024]{0:T(1024)S(1)} %get-tuple-element.137, bf16[1024,4096]{1,0:T(8,128)(2,1)} %get-tuple-element.158.lhs_ref, bf16[1,4096,1024]{2,1,0:T(8,128)(2,1)} %all-gather.14.cloned.1.call-done, f32[1024]{0:T(1024)S(1)} %get-tuple-element.136, ...), kind=kOutput, calls=%fused_computation.46 | convolution fusion | flops 8598322176 | bytes 25178112 | tf_op jit(solution)/shard_map/dot_general | solution.py:55
  189.6 48.9 %all-gather.12.cloned.1.call-done.wq_ref.wk_ref.wv_ref = bf16[1024,8192]{1,0:T(8,128)(2,1)} async-done(((bf16[128,8192]{1,0:T(8,128)(2,1)}), bf16[1024,8192]{1,0:T(8,128)(2,1)}) %all-gather.12.cloned.1.call-update) | async-done | bytes 16777232 | tf_op jit(solution)/shard_map/all_gather | solution.py:300
  238.5 18.9 %multiply_convert_fusion = (bf16[1024,4096]{1,0:T(8,128)(2,1)}, f32[1024,4096]{1,0:T(8,128)}) fusion(f32[4096]{0:T(1024)S(1)} %bitcast.252, bf16[1024,1024]{1,0:T(8,128)(2,1)S(1)} %fusion.53.h_ref.refs_1_.refs_2_.refs_3_.refs_4_, bf16[1024,8192]{1,0:T(8,128)(2,1)} %all-gather.12.cloned.1.call-done.wq_ref.wk_ref.wv_ref), kind=kOutput, calls=%fused_computation.26 | convolution fusion | flops 8631877632 | bytes 35667968 | tf_op jit(solution)/shard_map/dot_general | solution.py:55
  258.0 20.5 %collective-permute-done.4.rhs2_ref.refs_20_ = bf16[1024,1024]{1,0:T(8,128)(2,1)} collective-permute-done((bf16[1024,1024]{1,0:T(8,128)(2,1)}, bf16[1024,1024]{1,0:T(8,128)(2,1)}, u32[]{:S(2)}, u32[]{:S(2)}) %collective-permute-start.4) | collective-permute-done | bytes 2097184 | tf_op jit(solution)/shard_map/ppermute | solution.py:297
  278.5 15.0 %wgrad_rows.2 = f32[2048,1024]{1,0:T(8,128)} custom-call(s32[1]{0:T(128)} %bitcast.19.core_ref.refs_0_, bf16[1024,4096]{1,0:T(8,128)(2,1)} %get-tuple-element.90.lhs_ref, bf16[1024,4096]{1,0:T(8,128)(2,1)} %collective-permute-done.3.lhs2_ref, bf16[1024,1024]{1,0:T(8,128)(2,1)} %bitcast.20.rhs_ref.refs_19_, ...), custom_call_target="tpu_custom_call" | custom-call | flops 8589934592 | bytes 20000000 | tf_op jit(solution)/shard_map/wgrad_rows/pallas_call | solution.py:190
  293.6 27.5 %fusion.136 = (f32[4096]{0:T(1024)}, bf16[1024,4096]{1,0:T(8,128)(2,1)}) fusion(f32[1024,4096]{1,0:T(8,128)} %get-tuple-element.163, f32[4096]{0:T(1024)S(1)} %bitcast.253, bf16[1024,1024]{1,0:T(8,128)(2,1)} %bitcast.20.rhs_ref.refs_19_, bf16[1,4096,1024]{2,1,0:T(8,128)(2,1)} %all-gather.16.cloned.1.call-done), kind=kOutput, calls=%fused_computation.229 | convolution fusion | flops 8690593792 | bytes 35684352 | tf_op jit(solution)/shard_map/dot_general | solution.py:51
  321.6 46.6 %attn_fwd.3 = (bf16[3,1024,1024]{2,1,0:T(8,128)(2,1)}, bf16[1024,1024]{1,0:T(8,128)(2,1)}, f32[4,8,1024]{2,1,0:T(8,128)}) custom-call(bf16[1024,1024]{1,0:T(8,128)(2,1)} %copy-done, bf16[1024,8192]{1,0:T(8,128)(2,1)} %all-gather.12.cloned.1.call-done.wq_ref.wk_ref.wv_ref, bf16[1024,8192]{1,0:T(8,128)(2,1)} %all-gather.12.cloned.1.call-done.wq_ref.wk_ref.wv_ref, ...), custom_call_target="tpu_custom_call" | custom-call | flops 20000000000 | bytes 20000000 | tf_op jit(solution)/shard_map/attn_fwd/pallas_call | solution.py:108
  368.3 16.4 %wgrad_cols.3 = f32[512,4096]{1,0:T(8,128)} custom-call(s32[1]{0:T(128)} %bitcast.19.core_ref.refs_0_, bf16[1024,1024]{1,0:T(8,128)(2,1)} %copy-done, bf16[1024,1024]{1,0:T(8,128)(2,1)} %copy-done, bf16[1024,1024]{1,0:T(8,128)(2,1)} %copy-done, bf16[1024,1024]{1,0:T(8,128)(2,1)} %copy-done, ...), custom_call_target="tpu_custom_call" | custom-call | flops 8589934592 | bytes 25600000 | tf_op jit(solution)/shard_map/wgrad_cols/pallas_call | solution.py:257
  390.7 48.2 %attn_bwd.2 = (bf16[3,1024,1024]{2,1,0:T(8,128)(2,1)}, f32[8,3072]{1,0:T(8,128)}) custom-call(bf16[3,1024,1024]{2,1,0:T(8,128)(2,1)} %get-tuple-element.68.qkv_ref, bf16[1024,1024]{1,0:T(8,128)(2,1)} %convolution_convert_fusion.1.go_ref, f32[4,8,1024]{2,1,0:T(8,128)} %get-tuple-element.73.lse_ref, f32[1024,256]{1,0:T(8,128)} %copy.159.keep_ref, ...), custom_call_target="tpu_custom_call" | custom-call | flops 49999998976 | bytes 20000000 | tf_op jit(solution)/shard_map/attn_bwd/pallas_call | solution.py:169
  439.4 15.3 %fusion.30 = f32[1024,1024]{1,0:T(8,128)} fusion(bf16[1024,4096]{1,0:T(8,128)(2,1)} %get-tuple-element.76.refs_9_, bf16[1024,8192]{1,0:T(8,128)(2,1)} %all-gather.12.cloned.1.call-done.wq_ref.wk_ref.wv_ref), kind=kOutput, calls=%fused_computation.36 | convolution fusion | flops 8589934592 | bytes 20971520 | tf_op jit(solution)/shard_map/dot_general | solution.py:51
  456.0 18.4 %wgrad_cols.4 = f32[512,4096]{1,0:T(8,128)} custom-call(s32[1]{0:T(128)} %bitcast.19.core_ref.refs_0_, bf16[1024,1024]{1,0:T(8,128)(2,1)} %copy-done, bf16[1024,1024]{1,0:T(8,128)(2,1)} %copy-done, bf16[1024,1024]{1,0:T(8,128)(2,1)} %copy-done, bf16[1024,1024]{1,0:T(8,128)(2,1)} %copy-done, ...), custom_call_target="tpu_custom_call" | custom-call | flops 8589934592 | bytes 25600000 | tf_op jit(solution)/shard_map/wgrad_cols/pallas_call | solution.py:257
  495.7 24.9 %fusion.135 = (f32[4096]{0:T(1024)S(1)}, bf16[1024,4096]{1,0:T(8,128)(2,1)}) fusion(f32[1024,4096]{1,0:T(8,128)} %get-tuple-element.159, f32[4096]{0:T(1024)S(1)} %bitcast.251, bf16[1024,1024]{1,0:T(8,128)(2,1)S(1)} %get-tuple-element.82.rhs_ref.refs_21_, bf16[1,4096,1024]{2,1,0:T(8,128)(2,1)} %all-gather.14.cloned.1.call-done), kind=kOutput, calls=%fused_computation.228 | convolution fusion | flops 8690593792 | bytes 35684352 | tf_op jit(solution)/shard_map/dot_general | solution.py:51
  520.5 15.4 %wgrad_rows.3 = f32[2048,1024]{1,0:T(8,128)} custom-call(s32[1]{0:T(128)} %bitcast.19.core_ref.refs_0_, bf16[1024,4096]{1,0:T(8,128)(2,1)} %get-tuple-element.158.lhs_ref, bf16[1024,4096]{1,0:T(8,128)(2,1)} %collective-permute-done.2.lhs2_ref, bf16[1024,1024]{1,0:T(8,128)(2,1)} %copy-done.10, bf16[1024,1024]{1,0:T(8,128)(2,1)} %collective-permute-done.9.rhs2_ref.refs_22_), custom_call_target="tpu_custom_call" | custom-call | flops 8589934592 | bytes 20000000 | tf_op jit(solution)/shard_map/wgrad_rows/pallas_call | solution.py:190
  543.0 48.4 %attn_bwd.3 = (bf16[3,1024,1024]{2,1,0:T(8,128)(2,1)}, f32[8,3072]{1,0:T(8,128)}) custom-call(bf16[3,1024,1024]{2,1,0:T(8,128)(2,1)} %get-tuple-element.60.qkv_ref, bf16[1024,1024]{1,0:T(8,128)(2,1)} %convolution_convert_fusion.go_ref, f32[4,8,1024]{2,1,0:T(8,128)} %get-tuple-element.83.lse_ref, f32[1024,256]{1,0:T(8,128)} %copy.159.keep_ref, ...), custom_call_target="tpu_custom_call" | custom-call | flops 49999998976 | bytes 20000000 | tf_op jit(solution)/shard_map/attn_bwd/pallas_call | solution.py:169
  592.0 15.5 %fusion.34 = f32[1024,1024]{1,0:T(8,128)} fusion(bf16[1024,4096]{1,0:T(8,128)(2,1)} %get-tuple-element.87.refs_19_, bf16[1024,8192]{1,0:T(8,128)(2,1)} %all-gather.10.cloned.1.call-done.wq_ref.wk_ref.wv_ref), kind=kOutput, calls=%fused_computation.40 | convolution fusion | flops 8589934592 | bytes 20971520 | tf_op jit(solution)/shard_map/dot_general | solution.py:51
  610.2 33.5 %wgrad_cols.5 = f32[512,8192]{1,0:T(8,128)} custom-call(s32[1]{0:T(128)} %bitcast.19.core_ref.refs_0_, bf16[1024,1024]{1,0:T(8,128)(2,1)} %fusion.60.h_ref.refs_1_.refs_2_.refs_3_.refs_4_, bf16[1024,1024]{1,0:T(8,128)(2,1)} %fusion.60.h_ref.refs_1_.refs_2_.refs_3_.refs_4_, bf16[1024,1024]{1,0:T(8,128)(2,1)} %fusion.60.h_ref.refs_1_.refs_2_.refs_3_.refs_4_, ...), custom_call_target="tpu_custom_call" | custom-call | flops 17179869184 | bytes 51200000 | tf_op jit(solution)/shard_map/wgrad_cols/pallas_call | solution.py:257
  660.1 7.6 fusion.64
  667.9 18.6 %all-gather.3 = f32[64,2,1280]{2,0,1:T(8,128)S(1)} all-gather(f32[8,2,1280]{2,0,1:T(8,128)S(1)} %pad_maximum_fusion.6), channel_id=5, replica_groups=mesh['fsdp'=8] {'fsdp'}, dimensions={0}, use_global_device_ids=true | all-gather | bytes 737280 | tf_op jit(solution)/shard_map/all_gather | solution.py:300
  695.1 12.6 %fusion.112 = bf16[1,1024,1024]{2,1,0:T(8,128)(2,1)} fusion(f32[1024]{0:T(1024)S(1)} %copy-done.47, bf16[1024,4096]{1,0:T(8,128)(2,1)} %get-tuple-element.90.lhs_ref, bf16[1,4096,1024]{2,1,0:T(8,128)(2,1)S(1)} %bitcast.268, f32[1024]{0:T(1024)S(1)} %copy-done.46, f32[1024,1024]{1,0:T(8,128)S(1)} %fusion.106, bf16[1024,1024]{1,0:T(8,128)(2,1)S(1)} %copy-done.15), kind=kOutput, calls=%fused_computation.135 | convolution fusion | flops 8596226048 | bytes 25174016 | tf_op jit(solution)/shard_map/dot_general | solution.py:55
  720.2 76.4 %reduce-scatter.6.cloned.1.call-done = f32[128,8192]{1,0:T(8,128)} async-done(((f32[512,8192]{1,0:T(8,128)}), f32[128,8192]{1,0:T(8,128)}) %reduce-scatter.6.cloned.1.call-update) | async-done | bytes 4194320 | tf_op jit(solution)/shard_map/reduce_scatter | solution.py:303
  (295 shorter events, 132.3 us)
Async XLA Ops:
  7.2 93.6 %all-gather.10.cloned.1.call-start = ((), (), s32[]{:S(2)}) async-start(), calls=%async_computation.5 | async-start | bytes 18874368 | tf_op jit(solution)/shard_map/all_gather | solution.py:300
  13.5 159.4 %all-gather.14.cloned.1.call-start = ((), (), s32[]{:S(2)}) async-start(), calls=%async_computation.12 | async-start | bytes 9437184 | tf_op jit(solution)/shard_map/all_gather | solution.py:300
  16.6 221.9 %all-gather.12.cloned.1.call-start = ((), (), s32[]{:S(2)}) async-start(), calls=%async_computation.6 | async-start | bytes 18874368 | tf_op jit(solution)/shard_map/all_gather | solution.py:300
  23.6 270.0 %all-gather.16.cloned.1.call-start = ((), (), s32[]{:S(2)}) async-start(), calls=%async_computation.13 | async-start | bytes 9437184 | tf_op jit(solution)/shard_map/all_gather | solution.py:300
  24.2 621.4 %reduce-scatter.14.cloned.1.call-start = ((), (), s32[]{:S(2)}) async-start(), calls=%async_computation.11 | async-start | bytes 10485760 | tf_op jit(solution)/shard_map/reduce_scatter | solution.py:303
  40.3 147.8 %copy-start.35 = (f32[1024]{0:T(1024)}, f32[1024]{0:T(1024)S(1)}, u32[]{:S(2)}) copy-start(f32[1024]{0:T(1024)S(1)} %get-tuple-element.135) | copy-start | bytes 12292
  189.6 131.6 %copy-start = (bf16[1024,1024]{1,0:T(8,128)(2,1)}, bf16[1024,1024]{1,0:T(8,128)(2,1)S(1)}, u32[]{:S(2)}) copy-start(bf16[1024,1024]{1,0:T(8,128)(2,1)S(1)} %fusion.53.h_ref.refs_1_.refs_2_.refs_3_.refs_4_) | copy-start | bytes 6291460
  257.5 21.0 %collective-permute-start.3 = (bf16[1024,4096]{1,0:T(8,128)(2,1)}, bf16[1024,4096]{1,0:T(8,128)(2,1)}, u32[]{:S(2)}, u32[]{:S(2)}) collective-permute-start(bf16[1024,4096]{1,0:T(8,128)(2,1)} %get-tuple-element.90.lhs_ref), channel_id=1, source_target_pairs={{0,1},{1,0},{2,3},{3,2},{4,5},{5,4},{6,7},{7,6}} | collective-permute-start | bytes 25165832 | tf_op jit(solution)/shard_map/ppermute | solution.py:297
  257.7 20.7 %collective-permute-start.4 = (bf16[1024,1024]{1,0:T(8,128)(2,1)}, bf16[1024,1024]{1,0:T(8,128)(2,1)}, u32[]{:S(2)}, u32[]{:S(2)}) collective-permute-start(bf16[1024,1024]{1,0:T(8,128)(2,1)} %bitcast.20.rhs_ref.refs_19_), channel_id=1, source_target_pairs={{0,1},{1,0},{2,3},{3,2},{4,5},{5,4},{6,7},{7,6}} | collective-permute-start | bytes 6291464 | tf_op jit(solution)/shard_map/ppermute | solution.py:297
  293.5 414.1 %reduce-scatter.10.cloned.1.call-start = ((), (), s32[]{:S(2)}) async-start(), calls=%async_computation.9 | async-start | bytes 10485760 | tf_op jit(solution)/shard_map/reduce_scatter | solution.py:303
  321.1 47.1 %collective-permute-start.6 = (bf16[1024,4096]{1,0:T(8,128)(2,1)}, bf16[1024,4096]{1,0:T(8,128)(2,1)}, u32[]{:S(2)}, u32[]{:S(2)}) collective-permute-start(bf16[1024,4096]{1,0:T(8,128)(2,1)} %get-tuple-element.76.refs_9_), channel_id=1, source_target_pairs={{0,1},{1,0},{2,3},{3,2},{4,5},{5,4},{6,7},{7,6}} | collective-permute-start | bytes 25165832 | tf_op jit(solution)/shard_map/ppermute | solution.py:297
  321.2 47.0 %collective-permute-start.5 = (bf16[1024,1024]{1,0:T(8,128)(2,1)S(1)}, bf16[1024,1024]{1,0:T(8,128)(2,1)}, u32[]{:S(2)}, u32[]{:S(2)}) collective-permute-start(bf16[1024,1024]{1,0:T(8,128)(2,1)S(1)} %fusion.53.h_ref.refs_1_.refs_2_.refs_3_.refs_4_), channel_id=1, source_target_pairs={{0,1},{1,0},{2,3},{3,2},{4,5},{5,4},{6,7},{7,6}} | collective-permute-start | bytes 6291464 | tf_op jit(solution)/shard_map/ppermute | solution.py:297
  384.8 326.0 %reduce-scatter.8.cloned.1.call-start = ((), (), s32[]{:S(2)}) async-start(), calls=%async_computation.8 | async-start | bytes 10485760 | tf_op jit(solution)/shard_map/reduce_scatter | solution.py:303
  438.9 17.2 %collective-permute-start.8 = (bf16[3,1024,1024]{2,1,0:T(8,128)(2,1)}, bf16[3,1024,1024]{2,1,0:T(8,128)(2,1)}, u32[]{:S(2)}, u32[]{:S(2)}) collective-permute-start(bf16[3,1024,1024]{2,1,0:T(8,128)(2,1)} %get-tuple-element.80.refs_17_), channel_id=1, source_target_pairs={{0,1},{1,0},{2,3},{3,2},{4,5},{5,4},{6,7},{7,6}} | collective-permute-start | bytes 18874376 | tf_op jit(solution)/shard_map/ppermute | solution.py:297
  438.9 15.8 %collective-permute-start.7 = (bf16[1024,1024]{1,0:T(8,128)(2,1)S(1)}, bf16[1024,1024]{1,0:T(8,128)(2,1)S(1)}, u32[]{:S(2)}, u32[]{:S(2)}) collective-permute-start(bf16[1024,1024]{1,0:T(8,128)(2,1)S(1)} %copy-done.3), channel_id=1, source_target_pairs={{0,1},{1,0},{2,3},{3,2},{4,5},{5,4},{6,7},{7,6}} | collective-permute-start | bytes 6291464 | tf_op jit(solution)/shard_map/ppermute | solution.py:297
  474.5 241.6 %reduce-scatter.12.cloned.1.call-start = ((), (), s32[]{:S(2)}) async-start(), calls=%async_computation.10 | async-start | bytes 10485760 | tf_op jit(solution)/shard_map/reduce_scatter | solution.py:303
  475.0 45.6 %collective-permute-start.2 = (bf16[1024,4096]{1,0:T(8,128)(2,1)}, bf16[1024,4096]{1,0:T(8,128)(2,1)}, u32[]{:S(2)}, u32[]{:S(2)}) collective-permute-start(bf16[1024,4096]{1,0:T(8,128)(2,1)} %get-tuple-element.158.lhs_ref), channel_id=1, source_target_pairs={{0,1},{1,0},{2,3},{3,2},{4,5},{5,4},{6,7},{7,6}} | collective-permute-start | bytes 25165832 | tf_op jit(solution)/shard_map/ppermute | solution.py:297
  495.7 24.9 %collective-permute-start.9 = (bf16[1024,1024]{1,0:T(8,128)(2,1)S(1)}, bf16[1024,1024]{1,0:T(8,128)(2,1)}, u32[]{:S(2)}, u32[]{:S(2)}) collective-permute-start(bf16[1024,1024]{1,0:T(8,128)(2,1)S(1)} %get-tuple-element.82.rhs_ref.refs_21_), channel_id=1, source_target_pairs={{0,1},{1,0},{2,3},{3,2},{4,5},{5,4},{6,7},{7,6}} | collective-permute-start | bytes 6291464 | tf_op jit(solution)/shard_map/ppermute | solution.py:297
  535.9 260.6 %reduce-scatter.6.cloned.1.call-start = ((), (), s32[]{:S(2)}) async-start(), calls=%async_computation.7 | async-start | bytes 20971520 | tf_op jit(solution)/shard_map/reduce_scatter | solution.py:303
  536.0 74.2 %collective-permute-start.11 = (bf16[1024,4096]{1,0:T(8,128)(2,1)}, bf16[1024,4096]{1,0:T(8,128)(2,1)}, u32[]{:S(2)}, u32[]{:S(2)}) collective-permute-start(bf16[1024,4096]{1,0:T(8,128)(2,1)} %get-tuple-element.87.refs_19_), channel_id=1, source_target_pairs={{0,1},{1,0},{2,3},{3,2},{4,5},{5,4},{6,7},{7,6}} | collective-permute-start | bytes 25165832 | tf_op jit(solution)/shard_map/ppermute | solution.py:297
  591.4 18.8 %collective-permute-start.10 = (bf16[3,1024,1024]{2,1,0:T(8,128)(2,1)}, bf16[3,1024,1024]{2,1,0:T(8,128)(2,1)}, u32[]{:S(2)}, u32[]{:S(2)}) collective-permute-start(bf16[3,1024,1024]{2,1,0:T(8,128)(2,1)} %get-tuple-element.92.refs_17_), channel_id=1, source_target_pairs={{0,1},{1,0},{2,3},{3,2},{4,5},{5,4},{6,7},{7,6}} | collective-permute-start | bytes 18874376 | tf_op jit(solution)/shard_map/ppermute | solution.py:297
  591.5 16.1 %collective-permute-start = (bf16[1024,1024]{1,0:T(8,128)(2,1)S(1)}, bf16[1024,1024]{1,0:T(8,128)(2,1)S(1)}, u32[]{:S(2)}, u32[]{:S(2)}) collective-permute-start(bf16[1024,1024]{1,0:T(8,128)(2,1)S(1)} %copy-done.2), channel_id=1, source_target_pairs={{0,1},{1,0},{2,3},{3,2},{4,5},{5,4},{6,7},{7,6}} | collective-permute-start | bytes 6291464 | tf_op jit(solution)/shard_map/ppermute | solution.py:297
  591.9 16.9 %collective-permute-start.1 = (bf16[1024,1024]{1,0:T(8,128)(2,1)}, bf16[1024,1024]{1,0:T(8,128)(2,1)S(1)}, u32[]{:S(2)}, u32[]{:S(2)}) collective-permute-start(bf16[1024,1024]{1,0:T(8,128)(2,1)} %get-tuple-element.59.refs_9_.refs_10_.refs_11_.refs_12_), channel_id=1, source_target_pairs={{0,1},{1,0},{2,3},{3,2},{4,5},{5,4},{6,7},{7,6}} | collective-permute-start | bytes 6291464 | tf_op jit(solution)/shard_map/ppermute | solution.py:297
  687.8 126.3 %copy-start.42 = (f32[2,128]{1,0:T(2,128)}, f32[2,128]{1,0:T(2,128)S(1)}, u32[]{:S(2)}) copy-start(f32[2,128]{1,0:T(2,128)S(1)} %get-tuple-element.202) | copy-start | bytes 3076
  (60 other events, 571.0 us)
Sparse Core Ops, SparseCore 0:
  13.6 87.1 all-gather.9
  103.2 48.6 all-gather.13
  154.3 84.1 all-gather.11
  240.8 48.6 all-gather.15
  293.7 80.7 reduce-scatter.13
  384.9 80.7 reduce-scatter.9
  474.6 81.3 reduce-scatter.7
  559.0 80.7 reduce-scatter.11
  644.0 152.5 reduce-scatter.5
